TPU v7x, 32 devices: a whole 2x2x4 slice. The times are simulated.
32 devices in a mesh: gx: 4 (over y, x), gy: 8 (over z, core).
Axes of the slice: x: 2, y: 2, z: 4, core: 2. Of those that a mesh axis runs over, the one named last changes fastest.
Arguments:
- facets: float32 [2048, 12, 128], P(('gx', 'gy')), may hold values from -6 to 6
- owner: int32 [2048, 1], P(('gx', 'gy')), may hold values from 0 to 31; in each aligned block of 64 rows (0 to 63, 64 to 127, ...) at most 4 rows name the same one
- ghosts: int32 [32, 16], P(('gx', 'gy')), may hold values from 0 to 2047, as said below
- ghost_count: int32 [32], P(('gx', 'gy')), may hold values from 1 to 16, 256 in all
- nodes: float32 [3, 16384], P(None, ('gx', 'gy')), may hold values from -6 to 6
- cand: int32 [4, 16384], P(None, ('gx', 'gy')), may hold values from 0 to 15
Outputs:
- own_gap: float32 [16384], P(('gx', 'gy'))
- ghost_gap: float32 [16384], P(('gx', 'gy'))
Inputs may be any that keep to these rules, and one draw needn't show every extreme that they name: Among the 64 blocks of one element-order device at most 4 have the same owner, and some owner reaches 4; every partition owns at least one block. `ghosts`: each row holds 16 distinct block ids. The blocks of element-order device h are h * 64 to h * 64 + 63; in every row exactly one device holds 2 of the entries and every other device holds at most one.
All inputs are finite; a program needn't handle non-finite values. No bound on the sum of `ghost_count` on one device may be relied on, other than what follows from the above.
Results may differ from a plain program's by a relative error of at most 0.0003.
Values sent between devices are 32-bit elements; how exact they have to be, the bound alone decides.
No kernel may reach another device: no remote copies, remote signals or barrier semaphores. Data moves between devices by JAX's collectives and lax.ppermute only.
A program may use at most 64 MiB of HBM per device.

v0:
```python
import math

import jax
import jax.numpy as jnp
from jax import lax
from jax.sharding import PartitionSpec as P

CAP = 4
GC = 2


far_gap = 10.0
penalty = 1e30


def facet_features(blocks, absent):
    vertex_a = blocks[:, 0:3]
    vertex_b = blocks[:, 3:6]
    vertex_c = blocks[:, 6:9]
    normal = blocks[:, 9:12]
    centre = (vertex_a + vertex_b + vertex_c) / 3.0
    spread = jnp.sum(vertex_a * vertex_a + vertex_b * vertex_b + vertex_c * vertex_c, axis=1) / 3.0
    offset = spread - jnp.sum(normal * vertex_a, axis=1) + penalty * absent[:, None]
    linear = normal - 2.0 * centre
    unit_row = jnp.ones_like(offset)
    stacked = jnp.concatenate([linear, unit_row[:, None], offset[:, None]], axis=1)
    return jnp.moveaxis(stacked, 1, 0).reshape(5, -1)


def node_features(points):
    square = jnp.sum(points * points, axis=0, keepdims=True)
    return jnp.concatenate([points, square, jnp.ones_like(square)], axis=0)


def pair_gaps(node_feat, facet_feat):
    return lax.dot_general(
        node_feat,
        facet_feat,
        (((0,), (0,)), ((), ())),
        precision=lax.Precision.HIGHEST,
        preferred_element_type=jnp.float32,
    )


def local(facets, owner, ghosts, ghost_count, nodes, cand):
    part_count = lax.axis_size(("gx", "gy"))
    blocks_dev = facets.shape[0]
    facet_width = facets.shape[2]
    nodes_dev = nodes.shape[1]
    capacity = CAP
    pair_slots = GC
    slot_count = part_count * capacity
    target = owner[:, 0]
    node_feat = node_features(nodes)
    position = jnp.arange(blocks_dev, dtype=jnp.int32)
    before = (target[:, None] == target[None, :]) & (position[None, :] < position[:, None])
    rank_in = jnp.sum(before.astype(jnp.int32), axis=1, dtype=jnp.int32)
    slot_of = target * capacity + rank_in
    outgoing = jnp.zeros((slot_count, 12, facet_width), jnp.float32).at[slot_of].set(facets)
    present = jnp.zeros((slot_count,), jnp.float32).at[slot_of].set(1.0)
    arrived, arrival_flags = (
        lax.all_to_all(
            outgoing.reshape(part_count, capacity, 12, facet_width),
            ("gx", "gy"),
            split_axis=0,
            concat_axis=0,
            tiled=True,
        ),
        lax.all_to_all(
            present.reshape(part_count, capacity),
            ("gx", "gy"),
            split_axis=0,
            concat_axis=0,
            tiled=True,
        ),
    )
    arrived = arrived.reshape(slot_count, 12, facet_width)
    absent = 1.0 - arrival_flags.reshape(slot_count)
    group_size = math.gcd(32, slot_count)
    rounds = slot_count // group_size

    def own_step(running, operands):
        pieces, missing = operands
        gap_block = pair_gaps(node_feat, facet_features(pieces, missing))
        return (jnp.minimum(running, jnp.min(gap_block, axis=1)), None)

    initial = jnp.full((nodes_dev,), penalty, jnp.float32)
    own_gap, unused = lax.scan(
        own_step,
        initial,
        (arrived.reshape(rounds, group_size, 12, facet_width), absent.reshape(rounds, group_size)),
    )
    wanted = ghosts[0]
    holder = wanted // blocks_dev
    local_row = wanted % blocks_dev
    entries = jnp.arange(wanted.shape[0], dtype=jnp.int32)
    slot_ids = jnp.arange(pair_slots, dtype=jnp.int32)
    earlier = (holder[:, None] == holder[None, :]) & (entries[None, :] < entries[:, None])
    order_in = jnp.sum(earlier.astype(jnp.int32), axis=1, dtype=jnp.int32)
    all_parts = jnp.arange(part_count, dtype=jnp.int32)
    select = (holder[None, None, :] == all_parts[:, None, None]) & (
        order_in[None, None, :] == slot_ids[None, :, None]
    )
    request = jnp.sum(select.astype(jnp.int32) * local_row[None, None, :], axis=2, dtype=jnp.int32)
    reply = lax.all_to_all(
        facets[lax.all_to_all(request, ("gx", "gy"), split_axis=0, concat_axis=0, tiled=True)],
        ("gx", "gy"),
        split_axis=0,
        concat_axis=0,
        tiled=True,
    )
    fetched = reply[holder, order_in]
    ghost_feat = facet_features(fetched, jnp.zeros((fetched.shape[0],), jnp.float32))
    gap_block = pair_gaps(node_feat, ghost_feat).reshape(nodes_dev, fetched.shape[0], facet_width)
    limit = ghost_count[0]
    active = jnp.any(
        (cand[:, :, None] == entries[None, None, :]) & (entries[None, None, :] < limit), axis=0
    )
    ghost_gap = jnp.minimum(
        far_gap, jnp.min(jnp.where(active[:, :, None], gap_block, penalty), axis=(1, 2))
    )
    return (own_gap, ghost_gap)


def solution(mesh):
    return jax.shard_map(
        local,
        mesh=mesh,
        in_specs=(
            P(("gx", "gy"), None, None),
            P(("gx", "gy"), None),
            P(("gx", "gy"), None),
            P(("gx", "gy")),
            P(None, ("gx", "gy")),
            P(None, ("gx", "gy")),
        ),
        out_specs=(P(("gx", "gy")), P(("gx", "gy"))),
        check_vma=False,
    )
```

profile of v0, /device:TPU:0, one launch (start us, length us, event | category | flops | bytes accessed | tf_op | source)
XLA Modules:
  0.0 99.3 jit_solution(10819551516194898591)
XLA Ops:
  0.6 0.7 and_select_fusion.3
  2.3 0.7 copy.35
  3.0 7.3 %all-to-all-start.2 = ((s32[32,1,2]{2,1,0:T(1,128)}), s32[32,1,2]{2,1,0:T(1,128)S(1)}, u32[]{:S(2)}, u32[]{:S(2)}) async-start(s32[32,1,2]{2,1,0:T(1,128)} %copy.35), calls=%async_computation.2 | async-start | bytes 32768 | tf_op jit(solution)/shard_map/all_to_all | solution.py:106
  10.3 0.9 convert_reduce_fusion
  11.3 0.7 fusion.14
  11.9 0.8 scatter_custom_fusion.1
  12.7 0.7 all_to_all.21
  13.4 4.1 %all-to-all-done.2 = s32[32,1,2]{2,1,0:T(1,128)S(1)} async-done(((s32[32,1,2]{2,1,0:T(1,128)}), s32[32,1,2]{2,1,0:T(1,128)S(1)}, u32[]{:S(2)}, u32[]{:S(2)}) %all-to-all-start.2) | async-done | bytes 288 | tf_op jit(solution)/shard_map/all_to_all | solution.py:106
  17.5 2.6 %all-to-all-start.1 = ((f32[32,1,4]{2,1,0:T(1,128)}), f32[32,1,4]{2,1,0:T(1,128)S(1)}, u32[]{:S(2)}, u32[]{:S(2)}) async-start(f32[32,1,4]{2,1,0:T(1,128)} %bitcast.5), calls=%async_computation.1 | async-start | bytes 32768 | tf_op jit(solution)/shard_map/all_to_all | solution.py:69
  20.4 2.3 %gather_fusion = f32[64,12,128]{2,0,1:T(8,128)S(1)} fusion(f32[64,12,128]{2,0,1:T(8,128)} %param.8, s32[1024]{0:T(1024)S(1)} %pad_clamp_fusion), kind=kCustom, calls=%fused_computation | custom fusion | bytes 786688 | tf_op jit(solution)/shard_map/gather | solution.py:106
  22.7 0.9 copy.38
  23.6 3.7 %all-to-all-done.1 = f32[32,1,4]{2,1,0:T(1,128)S(1)} async-done(((f32[32,1,4]{2,1,0:T(1,128)}), f32[32,1,4]{2,1,0:T(1,128)S(1)}, u32[]{:S(2)}, u32[]{:S(2)}) %all-to-all-start.1) | async-done | bytes 544 | tf_op jit(solution)/shard_map/all_to_all | solution.py:69
  27.3 2.6 %all-to-all-start.3 = ((f32[32,2,12,128]{3,1,2,0:T(2,128)}), f32[32,2,12,128]{3,1,2,0:T(2,128)S(1)}, u32[]{:S(2)}, u32[]{:S(2)}) async-start(f32[32,2,12,128]{3,1,2,0:T(2,128)} %copy.38), calls=%async_computation.3 | async-start | bytes 786432 | tf_op jit(solution)/shard_map/all_to_all | solution.py:105
  30.3 2.4 %scatter_fusion = f32[128,12,128]{2,1,0:T(8,128)S(1)} fusion(f32[128,12,128]{2,1,0:T(8,128)S(1)} %broadcast_in_dim.23, s32[64]{0:T(128)S(1)} %fusion.14, f32[64,12,128]{2,1,0:T(8,128)S(1)} %copy.30), kind=kCustom, calls=%fused_computation.2 | custom fusion | bytes 1179904 | tf_op jit(solution)/shard_map/scatter | solution.py:59
  32.8 1.2 %copy.31 = f32[32,4,12,128]{3,1,2,0:T(4,128)} copy(f32[32,4,12,128]{3,2,1,0:T(8,128)S(1)} %bitcast.95) | data formatting | bytes 1572864 | tf_op jit(solution)/shard_map/reshape | solution.py:63
  34.8 8.5 %all-to-all-done.3 = f32[32,2,12,128]{3,1,2,0:T(2,128)S(1)} async-done(((f32[32,2,12,128]{3,1,2,0:T(2,128)}), f32[32,2,12,128]{3,1,2,0:T(2,128)S(1)}, u32[]{:S(2)}, u32[]{:S(2)}) %all-to-all-start.3) | async-done | bytes 393248 | tf_op jit(solution)/shard_map/all_to_all | solution.py:105
  43.3 2.6 %all-to-all-start = ((f32[32,4,12,128]{3,1,2,0:T(4,128)}), f32[32,4,12,128]{3,1,2,0:T(4,128)S(1)}, u32[]{:S(2)}, u32[]{:S(2)}) async-start(f32[32,4,12,128]{3,1,2,0:T(4,128)} %copy.31), calls=%async_computation | async-start | bytes 1572864 | tf_op jit(solution)/shard_map/all_to_all | solution.py:62
  47.0 3.9 %select_reduce_fusion = f32[512]{0:T(512)S(1)} fusion(pred[512,16]{0,1:T(8,128)(4,1)S(1)} %fusion.6, f32[16,1,128]{2,1,0:T(1,128)S(1)} %bitcast.99, f32[16,3,128]{2,1,0:T(4,128)S(1)} %get-tuple-element.111, f32[5]{0:T(128)S(1)} %pad.4.clone, f32[1,512]{1,0:T(1,128)S(1)} %bitcast.101, f32[3,512]{1,0:T(4,128)S(1)} %copy-done.2, f32[5]{0:T(128)S(1)} %pad.8.clone), kind=kOutput, calls=%fused_computation.20 | convolution fusion | flops 65036800 | bytes 51240 | tf_op jit(solution)/shard_map/dot_general | solution.py:36
  51.5 16.3 %all-to-all-done = f32[32,4,12,128]{3,1,2,0:T(4,128)S(1)} async-done(((f32[32,4,12,128]{3,1,2,0:T(4,128)}), f32[32,4,12,128]{3,1,2,0:T(4,128)S(1)}, u32[]{:S(2)}, u32[]{:S(2)}) %all-to-all-start) | async-done | bytes 786464 | tf_op jit(solution)/shard_map/all_to_all | solution.py:62
  68.0 30.7 %while.13 = (s32[]{:T(128)}, f32[512]{0:T(512)S(1)}, f32[4,32,12,128]{3,1,0,2:T(8,128)S(1)}, f32[4,32]{1,0:T(4,128)S(1)}, f32[5,512]{1,0:T(8,128)S(1)}, /*index=5*/s32[]{:T(128)}, f32[]{:T(128)}, f32[]{:T(128)}, s32[]{:T(128)}) while((s32[]{:T(128)}, f32[512]{0:T(512)S(1)}, f32[4,32,12,128]{3,1,0,2:T(8,128)S(1)}, ...), condition=%wide.region_8.9_spmd.clone, body=%wide.region_4.8_spmd.clone.sunk | while | flops 128119328 | bytes 1231399 | solution.py:88
  68.5 7.1 %convolution_reduce_fusion.2 = f32[512]{0:T(512)S(1)} fusion(f32[5,512]{1,0:T(8,128)S(1)} %get-tuple-element.173, f32[32,1,128]{2,1,0:T(1,128)S(1)} %broadcast_add_fusion.2, f32[32,3,128]{2,1,0:T(4,128)S(1)} %get-tuple-element.150, f32[5]{0:T(128)S(1)} %pad.1.clone.2), kind=kOutput, calls=%fused_computation.4.clone.1 | convolution fusion | flops 127966720 | bytes 77844 | tf_op jit(solution)/shard_map/while/body/eval_jaxpr/dot_general | solution.py:36
  76.2 7.1 %convolution_reduce_fusion.2 = f32[512]{0:T(512)S(1)} fusion(f32[5,512]{1,0:T(8,128)S(1)} %get-tuple-element.173, f32[32,1,128]{2,1,0:T(1,128)S(1)} %broadcast_add_fusion.2, f32[32,3,128]{2,1,0:T(4,128)S(1)} %get-tuple-element.150, f32[5]{0:T(128)S(1)} %pad.1.clone.2), kind=kOutput, calls=%fused_computation.4.clone.1 | convolution fusion | flops 127966720 | bytes 77844 | tf_op jit(solution)/shard_map/while/body/eval_jaxpr/dot_general | solution.py:36
  83.8 7.1 %convolution_reduce_fusion.2 = f32[512]{0:T(512)S(1)} fusion(f32[5,512]{1,0:T(8,128)S(1)} %get-tuple-element.173, f32[32,1,128]{2,1,0:T(1,128)S(1)} %broadcast_add_fusion.2, f32[32,3,128]{2,1,0:T(4,128)S(1)} %get-tuple-element.150, f32[5]{0:T(128)S(1)} %pad.1.clone.2), kind=kOutput, calls=%fused_computation.4.clone.1 | convolution fusion | flops 127966720 | bytes 77844 | tf_op jit(solution)/shard_map/while/body/eval_jaxpr/dot_general | solution.py:36
  91.5 7.1 %convolution_reduce_fusion.2 = f32[512]{0:T(512)S(1)} fusion(f32[5,512]{1,0:T(8,128)S(1)} %get-tuple-element.173, f32[32,1,128]{2,1,0:T(1,128)S(1)} %broadcast_add_fusion.2, f32[32,3,128]{2,1,0:T(4,128)S(1)} %get-tuple-element.150, f32[5]{0:T(128)S(1)} %pad.1.clone.2), kind=kOutput, calls=%fused_computation.4.clone.1 | convolution fusion | flops 127966720 | bytes 77844 | tf_op jit(solution)/shard_map/while/body/eval_jaxpr/dot_general | solution.py:36
  (71 shorter events, 6.1 us)
Async XLA Ops:
  3.0 14.5 %all-to-all-start.2 = ((s32[32,1,2]{2,1,0:T(1,128)}), s32[32,1,2]{2,1,0:T(1,128)S(1)}, u32[]{:S(2)}, u32[]{:S(2)}) async-start(s32[32,1,2]{2,1,0:T(1,128)} %copy.35), calls=%async_computation.2 | async-start | bytes 32768 | tf_op jit(solution)/shard_map/all_to_all | solution.py:106
  17.5 9.7 %all-to-all-start.1 = ((f32[32,1,4]{2,1,0:T(1,128)}), f32[32,1,4]{2,1,0:T(1,128)S(1)}, u32[]{:S(2)}, u32[]{:S(2)}) async-start(f32[32,1,4]{2,1,0:T(1,128)} %bitcast.5), calls=%async_computation.1 | async-start | bytes 32768 | tf_op jit(solution)/shard_map/all_to_all | solution.py:69
  22.7 7.2 %copy-start = (f32[64,12,128]{2,0,1:T(8,128)S(1)}, f32[64,12,128]{2,0,1:T(8,128)}, u32[]{:S(2)}) copy-start(f32[64,12,128]{2,0,1:T(8,128)} %param.8) | copy-start | bytes 1179652
  27.3 16.0 %all-to-all-start.3 = ((f32[32,2,12,128]{3,1,2,0:T(2,128)}), f32[32,2,12,128]{3,1,2,0:T(2,128)S(1)}, u32[]{:S(2)}, u32[]{:S(2)}) async-start(f32[32,2,12,128]{3,1,2,0:T(2,128)} %copy.38), calls=%async_computation.3 | async-start | bytes 786432 | tf_op jit(solution)/shard_map/all_to_all | solution.py:105
  32.8 1.9 %copy-start.3 = (s32[4,512]{1,0:T(4,128)S(1)}, s32[4,512]{1,0:T(4,128)}, u32[]{:S(2)}) copy-start(s32[4,512]{1,0:T(4,128)} %param.13) | copy-start | bytes 24580
  34.0 11.9 %copy-start.2 = (f32[3,512]{1,0:T(4,128)S(1)}, f32[3,512]{1,0:T(4,128)}, u32[]{:S(2)}) copy-start(f32[3,512]{1,0:T(4,128)} %param.12) | copy-start | bytes 18436
  34.0 12.0 %copy-start.4 = (s32[1,16]{1,0:T(1,128)S(1)}, s32[1,16]{1,0:T(1,128)}, u32[]{:S(2)}) copy-start(s32[1,16]{1,0:T(1,128)} %param.10) | copy-start | bytes 196
  43.3 24.5 %all-to-all-start = ((f32[32,4,12,128]{3,1,2,0:T(4,128)}), f32[32,4,12,128]{3,1,2,0:T(4,128)S(1)}, u32[]{:S(2)}, u32[]{:S(2)}) async-start(f32[32,4,12,128]{3,1,2,0:T(4,128)} %copy.31), calls=%async_computation | async-start | bytes 1572864 | tf_op jit(solution)/shard_map/all_to_all | solution.py:62
  98.7 0.6 copy-start.1
where the time goes:
time: 99.7 us; the launch traced here: 99.3 us
  waiting for transfers between devices  32.6 us (33%)
  matrix products  32.4 us (32%)
  starting transfers between devices  15.1 us (15%)
  local copies, waits for them, and re-layouts  12.1 us (12%)
  other arithmetic  5.25 us (5%)
  between operations  1.54 us (2%)
    dot_general x5, matrix products, pair_gaps(): lax.dot_general(node_feat, facet_feat, (((0,), (0,)), ((), ())), precisio...  32.4 us
    all_to_all x1, waiting for transfers between devices, local(): lax.all_to_all(outgoing.reshape(part_count, capacity, 12, facet_width), (...  16.3 us
    all_to_all x1, waiting for transfers between devices, local(): lax.all_to_all(facets[lax.all_to_all(request, ('gx', 'gy'), split_axis=0,...  8.5 us
    all_to_all x1, starting transfers between devices, local(): lax.all_to_all(request, ('gx', 'gy'), split_axis=0, concat_axis=0, tiled=...  7.33 us
    all_to_all x1, waiting for transfers between devices, local(): lax.all_to_all(request, ('gx', 'gy'), split_axis=0, concat_axis=0, tiled=...  4.11 us
    all_to_all x1, waiting for transfers between devices, local(): lax.all_to_all(present.reshape(part_count, capacity), ('gx', 'gy'), split...  3.68 us
    gather x2, local copies, waits for them, and re-layouts, local(): facets[lax.all_to_all(request, ('gx', 'gy'), split_axis=0, concat_axis=0,...  3.17 us
    all_to_all x1, starting transfers between devices, local(): lax.all_to_all(outgoing.reshape(part_count, capacity, 12, facet_width), (...  2.62 us
  transfers between devices with their start and end apart: 4, of which 4 were waited for; matrix products, arithmetic and copies ran while one was open for 16% of the time, Pallas kernels for 0%

commit v1 on v0

v1 whole, which is shorter than its diff:
```python
import jax
import jax.numpy as jnp
from jax import lax
from jax.experimental import pallas as pl
from jax.experimental.pallas import tpu as pltpu
from jax.sharding import PartitionSpec as P

CAP = 4
GC = 2
FEAT = 4
OWN_ROWS = CAP * FEAT
SEND_ROWS = OWN_ROWS + 1
REPLY_ROWS = GC * FEAT
AXES = ("gx", "gy")

far_gap = 10.0
penalty = 1e30


def split3(value):
    high = value.astype(jnp.bfloat16)
    rest = value - high.astype(jnp.float32)
    middle = rest.astype(jnp.bfloat16)
    low = (rest - middle.astype(jnp.float32)).astype(jnp.bfloat16)
    return high, middle, low


def to_one(flag):
    return jnp.where(flag, 1.0, 0.0)


def pack_kernel(facets_ref, owner_ref, ghosts_ref, out_ref, feat_ref):
    _, blocks, width = facets_ref.shape
    parts = out_ref.shape[0] // SEND_ROWS
    ax, ay, az, bx, by, bz, cx, cy, cz, nx, ny, nz = [facets_ref[i] for i in range(12)]
    third = 1.0 / 3.0
    squares = lambda u, v, w: u * u + v * v + w * w
    spread = (squares(ax, bx, cx) + squares(ay, by, cy) + squares(az, bz, cz)) * third
    offset = spread - (nx * ax + ny * ay + nz * az)
    feats = [n - (2.0 * third) * (a + b + c) for n, a, b, c in ((nx, ax, bx, cx), (ny, ay, by, cy), (nz, az, bz, cz))]
    feats.append(offset)
    splits = [split3(f) for f in feats]
    table = jnp.concatenate(
        [jnp.concatenate([splits[c][i] for c in range(FEAT)], axis=1) for i in range(3)], axis=0
    )
    feat_ref[...] = table

    owner_row = owner_ref[...]
    row_id = lax.broadcasted_iota(jnp.int32, (blocks, blocks), 0)
    col_id = lax.broadcasted_iota(jnp.int32, (blocks, blocks), 1)
    owner_col = jnp.sum(jnp.where(row_id == col_id, owner_row, 0), axis=1, keepdims=True)
    earlier = (owner_col == owner_row) & (row_id < col_id)
    rank = jnp.sum(jnp.where(earlier, 1, 0), axis=0, keepdims=True)
    part_id = lax.broadcasted_iota(jnp.int32, (parts, blocks), 0)
    mine = owner_row == part_id
    picks = [to_one(mine & (rank == s)) for s in range(CAP)]
    pick = jnp.concatenate(picks, axis=0).astype(jnp.bfloat16)
    placed = jnp.dot(jnp.concatenate([pick] * 3, axis=1), table, preferred_element_type=jnp.float32)
    for s in range(CAP):
        absent = 1.0 - jnp.sum(picks[s], axis=1, keepdims=True)
        for c in range(FEAT):
            piece = placed[s * parts : (s + 1) * parts, c * width : (c + 1) * width]
            if c == FEAT - 1:
                piece = piece + penalty * absent
            out_ref[pl.ds(s * FEAT + c, parts, stride=SEND_ROWS), :] = piece

    wanted = ghosts_ref[...]
    entries = wanted.shape[1]
    part_of = lax.broadcasted_iota(jnp.int32, (parts, entries), 0)
    entry = lax.broadcasted_iota(jnp.int32, (parts, entries), 1)
    holder = wanted // blocks
    local_row = wanted - holder * blocks
    held = part_of == holder
    first = jnp.min(jnp.where(held, entry, entries), axis=1, keepdims=True)
    last = jnp.max(jnp.where(held, entry, -1), axis=1, keepdims=True)
    row_first = jnp.sum(jnp.where(held & (entry == first), local_row, 0), axis=1, keepdims=True)
    row_last = jnp.sum(jnp.where(held & (entry == last), local_row, 0), axis=1, keepdims=True)
    lane = lax.broadcasted_iota(jnp.int32, (parts, width), 1)
    request = jnp.where(lane == 0, row_first, jnp.where(lane == 1, row_last, 0))
    out_ref[pl.ds(OWN_ROWS, parts, stride=SEND_ROWS), :] = request.astype(jnp.float32)


def select_kernel(arrived_ref, feat_ref, out_ref):
    parts = arrived_ref.shape[0] // SEND_ROWS
    width = arrived_ref.shape[1]
    blocks = feat_ref.shape[0] // 3
    request = arrived_ref[pl.ds(OWN_ROWS, parts, stride=SEND_ROWS), :].astype(jnp.int32)
    block_id = lax.broadcasted_iota(jnp.int32, (parts, blocks), 1)
    pick = jnp.concatenate([to_one(request[:, s : s + 1] == block_id) for s in range(GC)], axis=0)
    pick = pick.astype(jnp.bfloat16)
    rows = jnp.dot(jnp.concatenate([pick] * 3, axis=1), feat_ref[...], preferred_element_type=jnp.float32)
    for s in range(GC):
        for c in range(FEAT):
            out_ref[pl.ds(s * FEAT + c, parts, stride=REPLY_ROWS), :] = rows[
                s * parts : (s + 1) * parts, c * width : (c + 1) * width
            ]


def own_kernel(arrived_ref, nodes_ref, out_ref, spread_ref, best_ref):
    parts = arrived_ref.shape[0] // SEND_ROWS
    width = arrived_ref.shape[1]
    count = nodes_ref.shape[1]
    for c in range(3):
        for g in range(count // width):
            row = nodes_ref[c : c + 1, g * width : (g + 1) * width]
            spread_ref[c, g * width : (g + 1) * width, :] = jnp.broadcast_to(row, (width, width)).T
    chunk = 64

    def one_chunk(j, carry):
        start = pl.multiple_of(j * chunk, chunk)
        x, y, z = [spread_ref[c, pl.ds(start, chunk), :] for c in range(3)]

        def one_source(d, best):
            base = d * SEND_ROWS
            for s in range(CAP):
                lx, ly, lz, off = [arrived_ref[pl.ds(base + s * FEAT + c, 1), :] for c in range(FEAT)]
                best = jnp.minimum(best, (x * lx + y * ly) + (z * lz + off))
            return best

        best_ref[pl.ds(start, chunk), :] = lax.fori_loop(
            0, parts, one_source, jnp.full((chunk, width), penalty, jnp.float32)
        )
        return carry

    lax.fori_loop(0, count // chunk, one_chunk, 0)
    for g in range(count // width):
        here = slice(g * width, (g + 1) * width)
        least = jnp.min(best_ref[here, :].T, axis=0, keepdims=True)
        px, py, pz = [nodes_ref[c : c + 1, here] for c in range(3)]
        out_ref[:, here] = least + (px * px + py * py + pz * pz)


def ghost_kernel(place_ref, limit_ref, reply_ref, nodes_ref, cand_ref, out_ref, got_ref, mask_ref):
    entries = place_ref.shape[0]
    width = reply_ref.shape[1]
    count = nodes_ref.shape[1]
    groups = count // width
    for e in range(entries):
        got_ref[e * FEAT : (e + 1) * FEAT, :] = reply_ref[pl.ds(place_ref[e], FEAT), :]
    entry = lax.broadcasted_iota(jnp.int32, (entries, count), 0)
    chosen = entry == cand_ref[0:1, :]
    for k in range(1, cand_ref.shape[0]):
        chosen = chosen | (entry == cand_ref[k : k + 1, :])
    mask_ref[...] = jnp.where(chosen & (entry < limit_ref[0]), -penalty, penalty)
    turned = got_ref[...].T
    points = [
        [jnp.broadcast_to(nodes_ref[c : c + 1, g * width : (g + 1) * width], (8, width)) for g in range(groups)]
        for c in range(3)
    ]
    total = [jnp.full((8, width), penalty, jnp.float32) for _ in range(groups)]
    for e in range(entries):
        best = [None] * groups
        for f in range(width // 8):
            lx, ly, lz, off = [
                jnp.broadcast_to(turned[f * 8 : (f + 1) * 8, e * FEAT + c : e * FEAT + c + 1], (8, width))
                for c in range(FEAT)
            ]
            for g in range(groups):
                gap = (points[0][g] * lx + points[1][g] * ly) + (points[2][g] * lz + off)
                best[g] = gap if best[g] is None else jnp.minimum(best[g], gap)
        for g in range(groups):
            masked = jnp.maximum(best[g], mask_ref[e : e + 1, g * width : (g + 1) * width])
            total[g] = jnp.minimum(total[g], masked)
    for g in range(groups):
        here = slice(g * width, (g + 1) * width)
        least = jnp.min(total[g], axis=0, keepdims=True)
        px, py, pz = [nodes_ref[c : c + 1, here] for c in range(3)]
        out_ref[:, here] = jnp.minimum(far_gap, least + (px * px + py * py + pz * pz))


def exchange(rows, parts):
    per_part = rows.shape[0] // parts
    shaped = rows.reshape(parts, per_part, 1, rows.shape[1])
    moved = lax.all_to_all(shaped, AXES, split_axis=0, concat_axis=0, tiled=True)
    return moved.reshape(rows.shape)


def local(facets, owner, ghosts, ghost_count, nodes, cand):
    parts = lax.axis_size(AXES)
    blocks, _, width = facets.shape
    count = nodes.shape[1]
    entries = ghosts.shape[1]
    f32 = jnp.float32
    outgoing, table = pl.pallas_call(
        pack_kernel,
        out_shape=(
            jax.ShapeDtypeStruct((parts * SEND_ROWS, width), f32),
            jax.ShapeDtypeStruct((3 * blocks, FEAT * width), jnp.bfloat16),
        ),
        name="pack",
    )(jnp.transpose(facets, (1, 0, 2)), owner.T, ghosts)
    arrived = exchange(outgoing, parts)
    answer = pl.pallas_call(
        select_kernel, out_shape=jax.ShapeDtypeStruct((parts * REPLY_ROWS, width), f32), name="select"
    )(arrived, table)
    reply = exchange(answer, parts)
    own_gap = pl.pallas_call(
        own_kernel,
        out_shape=jax.ShapeDtypeStruct((1, count), f32),
        scratch_shapes=[pltpu.VMEM((3, count, width), f32), pltpu.VMEM((count, width), f32)],
        name="own",
        cost_estimate=pl.CostEstimate(
            flops=7 * parts * CAP * width * count, bytes_accessed=parts * SEND_ROWS * width * 4, transcendentals=0
        ),
    )(arrived, nodes)
    wanted = ghosts[0]
    holder = wanted // blocks
    entry = jnp.arange(entries, dtype=jnp.int32)
    before = (holder[:, None] == holder[None, :]) & (entry[None, :] < entry[:, None])
    order = jnp.sum(before.astype(jnp.int32), axis=1, dtype=jnp.int32)
    place = (holder * GC + order) * FEAT
    smem = pl.BlockSpec(memory_space=pltpu.SMEM)
    vmem = pl.BlockSpec(memory_space=pltpu.VMEM)
    ghost_gap = pl.pallas_call(
        ghost_kernel,
        out_shape=jax.ShapeDtypeStruct((1, count), f32),
        in_specs=[smem, smem, vmem, vmem, vmem],
        scratch_shapes=[pltpu.VMEM((entries * FEAT, width), f32), pltpu.VMEM((entries, count), f32)],
        name="ghost",
    )(place, ghost_count, reply, nodes, cand)
    return own_gap.reshape(count), ghost_gap.reshape(count)


def solution(mesh):
    return jax.shard_map(
        local,
        mesh=mesh,
        in_specs=(
            P(AXES, None, None),
            P(AXES, None),
            P(AXES, None),
            P(AXES),
            P(None, AXES),
            P(None, AXES),
        ),
        out_specs=(P(AXES), P(AXES)),
        check_vma=False,
    )
```

time: 99.7 us -> 42.4 us (0.43)
  matrix products: 32.4 us -> 0 us
  waiting for transfers between devices: 32.6 us -> 10.6 us
  Pallas kernels: 0 us -> 18.1 us
  local copies, waits for them, and re-layouts: 12.1 us -> 1.35 us
  starting transfers between devices: 15.1 us -> 9.96 us
  other arithmetic: 5.25 us -> 0.76 us
    dot_general x5 -> x0, matrix products: 32.4 us -> none  [pair_gaps(): lax.dot_general(node_feat, facet_feat, (((0,), (0,)), ((), ())), precisio...]
    all_to_all x4 -> x2, waiting for transfers between devices: 32.6 us -> 10.6 us  [exchange(): lax.all_to_all(shaped, AXES, split_axis=0, concat_axis=0, tiled=True)]
    pallas_call x0 -> x4, Pallas kernels: none -> 18.1 us  [the longest x1 10.5 us: local(): pl.pallas_call(own_kernel, out_shape=jax.ShapeDtypeStruct((1, count), f32...]
    all_to_all x4 -> x2, starting transfers between devices: 15.1 us -> 9.96 us  [exchange(): lax.all_to_all(shaped, AXES, split_axis=0, concat_axis=0, tiled=True)]
    gather x3 -> x0, local copies, waits for them, and re-layouts: 3.77 us -> none  [the longest x2 3.17 us: local(): facets[lax.all_to_all(request, ('gx', 'gy'), split_axis=0, concat_axis=0,...]
    scatter x2 -> x0, local copies, waits for them, and re-layouts: 3.21 us -> none  [the longest x1 2.44 us: local(): jnp.zeros((slot_count, 12, facet_width), jnp.float32).at[slot_of]]
    all_to_all x5 -> x0, local copies, waits for them, and re-layouts: 1.72 us -> none  [the longest x2 0.77 us: local(): lax.all_to_all(request, ('gx', 'gy'), split_axis=0, concat_axis=0, tiled=...]
    reduce_sum x9 -> x1, other arithmetic: 1.84 us -> 0.18 us  [local(): order = jnp.sum(before.astype(jnp.int32), axis=1, dtype=jnp.int32)]
  transfers between devices with their start and end apart: 4 -> 2, of which waited for: 4 -> 1; matrix products, arithmetic and copies ran while one was open for 16% -> 2% of each run, Pallas kernels for 0% -> 25%
where the time goes in v1:
time: 42.4 us; the launch traced here: 42.1 us
  Pallas kernels  18.1 us (43%)
  waiting for transfers between devices  10.6 us (25%)
  starting transfers between devices  9.96 us (23%)
  local copies, waits for them, and re-layouts  1.35 us (3%)
  between operations  1.33 us (3%)
  other arithmetic  0.76 us (2%)
    all_to_all x2, waiting for transfers between devices, exchange(): lax.all_to_all(shaped, AXES, split_axis=0, concat_axis=0, tiled=True)  10.6 us
    pallas_call x1, Pallas kernels, local(): pl.pallas_call(own_kernel, out_shape=jax.ShapeDtypeStruct((1, count), f32...  10.5 us
    all_to_all x2, starting transfers between devices, exchange(): lax.all_to_all(shaped, AXES, split_axis=0, concat_axis=0, tiled=True)  9.96 us
    pallas_call x1, Pallas kernels, local(): pl.pallas_call(ghost_kernel, out_shape=jax.ShapeDtypeStruct((1, count), f...  3.56 us
    pallas_call x1, Pallas kernels, local(): pl.pallas_call(pack_kernel, out_shape=(jax.ShapeDtypeStruct((parts * SEND...  2.13 us
    pallas_call x1, Pallas kernels, local(): pl.pallas_call(select_kernel, out_shape=jax.ShapeDtypeStruct((parts * REP...  1.94 us
    unnamed x6, local copies, waits for them, and re-layouts  1.35 us
  transfers between devices with their start and end apart: 2, of which 1 were waited for; matrix products, arithmetic and copies ran while one was open for 2% of the time, Pallas kernels for 25%

profile of v1, /device:TPU:0, one launch (start us, length us, event | category | flops | bytes accessed | tf_op | source)
XLA Modules:
  0.0 42.1 jit_solution(5372546793839581476)
XLA Ops:
  0.6 2.1 %pack.1 = (f32[544,128]{1,0:T(8,128)}, bf16[192,512]{1,0:T(8,128)(2,1)}) custom-call(f32[12,64,128]{2,1,0:T(8,128)} %bitcast.26, s32[1,64]{1,0:T(1,128)} %bitcast.30, s32[1,16]{1,0:T(1,128)} %ghosts_ref.1), custom_call_target="tpu_custom_call" | custom-call | tf_op jit(solution)/shard_map/pack/pallas_call | solution.py:184
  2.8 0.0 copy-start.2
  2.8 7.3 %all-to-all-start = ((f32[32,17,1,128]{3,2,1,0:T(1,128)}), f32[32,17,1,128]{3,2,1,0:T(1,128)S(1)}, u32[]{:S(2)}, u32[]{:S(2)}) async-start(f32[32,17,1,128]{3,2,1,0:T(1,128)} %bitcast.27), calls=%async_computation | async-start | bytes 557056 | tf_op jit(solution)/shard_map/all_to_all | solution.py:174
  10.1 0.0 copy-done.2
  10.1 10.6 %all-to-all-done = f32[32,17,1,128]{3,2,1,0:T(1,128)S(1)} async-done(((f32[32,17,1,128]{3,2,1,0:T(1,128)}), f32[32,17,1,128]{3,2,1,0:T(1,128)S(1)}, u32[]{:S(2)}, u32[]{:S(2)}) %all-to-all-start) | async-done | bytes 278560 | tf_op jit(solution)/shard_map/all_to_all | solution.py:174
  20.7 0.0 copy-start
  20.7 0.7 %copy-done = f32[32,17,1,128]{3,2,1,0:T(1,128)} copy-done((f32[32,17,1,128]{3,2,1,0:T(1,128)}, f32[32,17,1,128]{3,2,1,0:T(1,128)S(1)}, u32[]{:S(2)}) %copy-start) | copy-done | bytes 278552
  21.4 1.9 %select.22 = f32[256,128]{1,0:T(8,128)} custom-call(f32[544,128]{1,0:T(8,128)} %bitcast.22, bf16[192,512]{1,0:T(8,128)(2,1)} %get-tuple-element.5.feat_ref), custom_call_target="tpu_custom_call" | custom-call | tf_op jit(solution)/shard_map/select/pallas_call | solution.py:193
  23.3 2.6 %all-to-all-start.1 = ((f32[32,8,1,128]{3,1,2,0:T(8,128)}), f32[32,8,1,128]{3,1,2,0:T(8,128)S(1)}, u32[]{:S(2)}, u32[]{:S(2)}) async-start(f32[32,8,1,128]{3,1,2,0:T(8,128)} %bitcast.24), calls=%async_computation.1 | async-start | bytes 262144 | tf_op jit(solution)/shard_map/all_to_all | solution.py:174
  26.0 0.2 convert_reduce_fusion
  26.8 0.6 %add_multiply_fusion.place_ref = s32[16]{0:T(128)} fusion(s32[16]{0:T(128)S(1)} %convert_reduce_fusion, s32[1,16]{1,0:T(1,128)S(1)} %copy-done.2), kind=kLoop, calls=%fused_computation.12 | loop fusion | flops 288 | bytes 192 | tf_op jit(solution)/shard_map/mul | solution.py:211
  27.4 10.5 %own.1 = f32[1,512]{1,0:T(1,128)} custom-call(f32[544,128]{1,0:T(8,128)} %bitcast.23, f32[3,512]{1,0:T(4,128)} %nodes_ref.3), custom_call_target="tpu_custom_call" | custom-call | flops 58720256 | bytes 278528 | tf_op jit(solution)/shard_map/own/pallas_call | solution.py:197
  37.9 0.0 all-to-all-done.1
  37.9 0.0 copy-start.1
  37.9 0.6 %copy-done.1 = f32[32,8,1,128]{3,1,2,0:T(8,128)} copy-done((f32[32,8,1,128]{3,1,2,0:T(8,128)}, f32[32,8,1,128]{3,1,2,0:T(8,128)S(1)}, u32[]{:S(2)}) %copy-start.1) | copy-done | bytes 131096
  38.5 3.6 %ghost.1 = f32[1,512]{1,0:T(1,128)} custom-call(s32[16]{0:T(128)} %add_multiply_fusion.place_ref, s32[1]{0:T(128)S(6)} %copy.12.limit_ref, f32[256,128]{1,0:T(8,128)} %bitcast.25, f32[3,512]{1,0:T(4,128)} %nodes_ref.3, s32[4,512]{1,0:T(4,128)} %cand_ref.1), custom_call_target="tpu_custom_call" | custom-call | tf_op jit(solution)/shard_map/ghost/pallas_call | solution.py:214
  (2 shorter events, 0.0 us)
Async XLA Ops:
  2.8 7.3 %copy-start.2 = (s32[1,16]{1,0:T(1,128)S(1)}, s32[1,16]{1,0:T(1,128)}, u32[]{:S(2)}) copy-start(s32[1,16]{1,0:T(1,128)} %ghosts_ref.1) | copy-start | bytes 196
  2.8 17.9 %all-to-all-start = ((f32[32,17,1,128]{3,2,1,0:T(1,128)}), f32[32,17,1,128]{3,2,1,0:T(1,128)S(1)}, u32[]{:S(2)}, u32[]{:S(2)}) async-start(f32[32,17,1,128]{3,2,1,0:T(1,128)} %bitcast.27), calls=%async_computation | async-start | bytes 557056 | tf_op jit(solution)/shard_map/all_to_all | solution.py:174
  20.7 0.7 %copy-start = (f32[32,17,1,128]{3,2,1,0:T(1,128)}, f32[32,17,1,128]{3,2,1,0:T(1,128)S(1)}, u32[]{:S(2)}) copy-start(f32[32,17,1,128]{3,2,1,0:T(1,128)S(1)} %all-to-all-done) | copy-start | bytes 835588
  23.3 14.6 %all-to-all-start.1 = ((f32[32,8,1,128]{3,1,2,0:T(8,128)}), f32[32,8,1,128]{3,1,2,0:T(8,128)S(1)}, u32[]{:S(2)}, u32[]{:S(2)}) async-start(f32[32,8,1,128]{3,1,2,0:T(8,128)} %bitcast.24), calls=%async_computation.1 | async-start | bytes 262144 | tf_op jit(solution)/shard_map/all_to_all | solution.py:174
  37.9 0.6 %copy-start.1 = (f32[32,8,1,128]{3,1,2,0:T(8,128)}, f32[32,8,1,128]{3,1,2,0:T(8,128)S(1)}, u32[]{:S(2)}) copy-start(f32[32,8,1,128]{3,1,2,0:T(8,128)S(1)} %all-to-all-done.1) | copy-start | bytes 393220

commit v2 on v1

--- a/solution.py
+++ b/solution.py
@@ -1,3 +1,5 @@
+import functools
+
 import jax
 import jax.numpy as jnp
 from jax import lax
@@ -96,76 +98,98 @@
             ]
 
 
-def own_kernel(arrived_ref, nodes_ref, out_ref, spread_ref, best_ref):
+def stack_terms(high, middle, low):
+    return [high, high, high, middle, middle, low]
+
+
+def point_terms(points):
+    four = jnp.concatenate([points, jnp.ones_like(points[0:1])], axis=0)
+    high, middle, low = [t.astype(jnp.float32) for t in split3(jnp.concatenate([four, four], axis=0))]
+    return [high, middle, low, high, middle, high]
+
+
+def own_kernel(limit_ref, arrived_ref, nodes_ref, cand_ref, out_ref, left_ref, spread_ref, best_ref):
     parts = arrived_ref.shape[0] // SEND_ROWS
     width = arrived_ref.shape[1]
     count = nodes_ref.shape[1]
-    for c in range(3):
-        for g in range(count // width):
-            row = nodes_ref[c : c + 1, g * width : (g + 1) * width]
-            spread_ref[c, g * width : (g + 1) * width, :] = jnp.broadcast_to(row, (width, width)).T
-    chunk = 64
-
-    def one_chunk(j, carry):
-        start = pl.multiple_of(j * chunk, chunk)
-        x, y, z = [spread_ref[c, pl.ds(start, chunk), :] for c in range(3)]
-
-        def one_source(d, best):
-            base = d * SEND_ROWS
-            for s in range(CAP):
-                lx, ly, lz, off = [arrived_ref[pl.ds(base + s * FEAT + c, 1), :] for c in range(FEAT)]
-                best = jnp.minimum(best, (x * lx + y * ly) + (z * lz + off))
-            return best
-
-        best_ref[pl.ds(start, chunk), :] = lax.fori_loop(
-            0, parts, one_source, jnp.full((chunk, width), penalty, jnp.float32)
-        )
-        return carry
-
-    lax.fori_loop(0, count // chunk, one_chunk, 0)
-    for g in range(count // width):
-        here = slice(g * width, (g + 1) * width)
-        least = jnp.min(best_ref[here, :].T, axis=0, keepdims=True)
-        px, py, pz = [nodes_ref[c : c + 1, here] for c in range(3)]
-        out_ref[:, here] = least + (px * px + py * py + pz * pz)
-
-
-def ghost_kernel(place_ref, limit_ref, reply_ref, nodes_ref, cand_ref, out_ref, got_ref, mask_ref):
-    entries = place_ref.shape[0]
-    width = reply_ref.shape[1]
-    count = nodes_ref.shape[1]
-    groups = count // width
-    for e in range(entries):
-        got_ref[e * FEAT : (e + 1) * FEAT, :] = reply_ref[pl.ds(place_ref[e], FEAT), :]
+    half = count // 2
+    entries = left_ref.shape[1] - 6 * 2 * FEAT
     entry = lax.broadcasted_iota(jnp.int32, (entries, count), 0)
     chosen = entry == cand_ref[0:1, :]
     for k in range(1, cand_ref.shape[0]):
         chosen = chosen | (entry == cand_ref[k : k + 1, :])
-    mask_ref[...] = jnp.where(chosen & (entry < limit_ref[0]), -penalty, penalty)
-    turned = got_ref[...].T
-    points = [
-        [jnp.broadcast_to(nodes_ref[c : c + 1, g * width : (g + 1) * width], (8, width)) for g in range(groups)]
-        for c in range(3)
-    ]
-    total = [jnp.full((8, width), penalty, jnp.float32) for _ in range(groups)]
+    mask = jnp.where(chosen & (entry < limit_ref[0]), 0.0, penalty)
+    left = jnp.concatenate(point_terms(nodes_ref[...]) + [mask], axis=0).T.astype(jnp.bfloat16)
+    left_ref[...] = left
+    for c in range(3):
+        for g in range(half // width):
+            row = nodes_ref[c : c + 1, half + g * width : half + (g + 1) * width]
+            spread_ref[c, g * width : (g + 1) * width, :] = jnp.broadcast_to(row, (width, width)).T
+    best_ref[...] = jnp.full((count, width), penalty, jnp.float32)
+    sublane = lax.broadcasted_iota(jnp.int32, (2 * FEAT, width), 0)
+    chunk = 64
+    unroll = 4
+
+    def some_sources(i, carry):
+        for u in range(unroll):
+            base = (i * unroll + u) * SEND_ROWS
+            sides = []
+            for t in range(CAP // 2):
+                tile = arrived_ref[pl.ds(base + t * 2 * FEAT, 2 * FEAT), :]
+                for part in range(2):
+                    kept = jnp.where((sublane >= FEAT) == (part == 1), tile, 0.0)
+                    rows = stack_terms(*split3(kept)) + [jnp.zeros((entries, width), jnp.bfloat16)]
+                    sides.append(jnp.concatenate(rows, axis=0))
+            gaps = jnp.dot(left_ref[0:half, :], jnp.concatenate(sides, axis=1), preferred_element_type=jnp.float32)
+            least = best_ref[0:half, :]
+            for s in range(CAP):
+                least = jnp.minimum(least, gaps[:, s * width : (s + 1) * width])
+            best_ref[0:half, :] = least
+            for j in range(half // chunk):
+                x, y, z = [spread_ref[c, j * chunk : (j + 1) * chunk, :] for c in range(3)]
+                here = slice(half + j * chunk, half + (j + 1) * chunk)
+                least = best_ref[here, :]
+                for s in range(CAP):
+                    lx, ly, lz, off = [arrived_ref[pl.ds(base + s * FEAT + c, 1), :] for c in range(FEAT)]
+                    least = jnp.minimum(least, (x * lx + y * ly) + (z * lz + off))
+                best_ref[here, :] = least
+        return carry
+
+    lax.fori_loop(0, parts // unroll, some_sources, 0)
+    finish(best_ref, nodes_ref, out_ref)
+
+
+def finish(best_ref, nodes_ref, out_ref, most=None):
+    width = best_ref.shape[1]
+    for g in range(nodes_ref.shape[1] // width):
+        here = slice(g * width, (g + 1) * width)
+        least = jnp.min(best_ref[here, :].T, axis=0, keepdims=True)
+        px, py, pz = [nodes_ref[c : c + 1, here] for c in range(3)]
+        gap = least + (px * px + py * py + pz * pz)
+        out_ref[:, here] = gap if most is None else jnp.minimum(most, gap)
+
+
+def ghost_kernel(wanted_ref, reply_ref, nodes_ref, left_ref, out_ref, best_ref, *, blocks):
+    entries = wanted_ref.shape[1]
+    width = reply_ref.shape[1]
+    holders = [wanted_ref[0, e] // blocks for e in range(entries)]
+    slot = lax.broadcasted_iota(jnp.int32, (2 * FEAT, width), 0) // FEAT
+    choice = lax.broadcasted_iota(jnp.int32, (entries, width), 0)
+    sides = []
     for e in range(entries):
-        best = [None] * groups
-        for f in range(width // 8):
-            lx, ly, lz, off = [
-                jnp.broadcast_to(turned[f * 8 : (f + 1) * 8, e * FEAT + c : e * FEAT + c + 1], (8, width))
-                for c in range(FEAT)
-            ]
-            for g in range(groups):
-                gap = (points[0][g] * lx + points[1][g] * ly) + (points[2][g] * lz + off)
-                best[g] = gap if best[g] is None else jnp.minimum(best[g], gap)
-        for g in range(groups):
-            masked = jnp.maximum(best[g], mask_ref[e : e + 1, g * width : (g + 1) * width])
-            total[g] = jnp.minimum(total[g], masked)
-    for g in range(groups):
-        here = slice(g * width, (g + 1) * width)
-        least = jnp.min(total[g], axis=0, keepdims=True)
-        px, py, pz = [nodes_ref[c : c + 1, here] for c in range(3)]
-        out_ref[:, here] = jnp.minimum(far_gap, least + (px * px + py * py + pz * pz))
+        order = 0
+        for before in range(e):
+            order = order + jnp.where(holders[before] == holders[e], 1, 0)
+        tile = reply_ref[pl.ds(pl.multiple_of(holders[e] * REPLY_ROWS, REPLY_ROWS), REPLY_ROWS), :]
+        kept = jnp.where(slot == order, tile, 0.0)
+        rows = stack_terms(*split3(kept)) + [to_one(choice == e).astype(jnp.bfloat16)]
+        sides.append(jnp.concatenate(rows, axis=0))
+    gaps = jnp.dot(left_ref[...], jnp.concatenate(sides, axis=1), preferred_element_type=jnp.float32)
+    least = gaps[:, 0:width]
+    for e in range(1, entries):
+        least = jnp.minimum(least, gaps[:, e * width : (e + 1) * width])
+    best_ref[...] = least
+    finish(best_ref, nodes_ref, out_ref, far_gap)
 
 
 def exchange(rows, parts):
@@ -181,6 +205,9 @@
     count = nodes.shape[1]
     entries = ghosts.shape[1]
     f32 = jnp.float32
+    smem = pl.BlockSpec(memory_space=pltpu.SMEM)
+    vmem = pl.BlockSpec(memory_space=pltpu.VMEM)
+    params = pltpu.CompilerParams(vmem_limit_bytes=16 * 1024 * 1024)
     outgoing, table = pl.pallas_call(
         pack_kernel,
         out_shape=(
@@ -188,36 +215,35 @@
             jax.ShapeDtypeStruct((3 * blocks, FEAT * width), jnp.bfloat16),
         ),
         name="pack",
+        compiler_params=params,
     )(jnp.transpose(facets, (1, 0, 2)), owner.T, ghosts)
     arrived = exchange(outgoing, parts)
     answer = pl.pallas_call(
-        select_kernel, out_shape=jax.ShapeDtypeStruct((parts * REPLY_ROWS, width), f32), name="select"
+        select_kernel, out_shape=jax.ShapeDtypeStruct((parts * REPLY_ROWS, width), f32), name="select", compiler_params=params
     )(arrived, table)
     reply = exchange(answer, parts)
-    own_gap = pl.pallas_call(
+    own_gap, left = pl.pallas_call(
         own_kernel,
-        out_shape=jax.ShapeDtypeStruct((1, count), f32),
-        scratch_shapes=[pltpu.VMEM((3, count, width), f32), pltpu.VMEM((count, width), f32)],
+        out_shape=(
+            jax.ShapeDtypeStruct((1, count), f32),
+            jax.ShapeDtypeStruct((count, 6 * 2 * FEAT + entries), jnp.bfloat16),
+        ),
+        in_specs=[smem, vmem, vmem, vmem],
+        scratch_shapes=[pltpu.VMEM((3, count // 2, width), f32), pltpu.VMEM((count, width), f32)],
         name="own",
+        compiler_params=params,
         cost_estimate=pl.CostEstimate(
             flops=7 * parts * CAP * width * count, bytes_accessed=parts * SEND_ROWS * width * 4, transcendentals=0
         ),
-    )(arrived, nodes)
-    wanted = ghosts[0]
-    holder = wanted // blocks
-    entry = jnp.arange(entries, dtype=jnp.int32)
-    before = (holder[:, None] == holder[None, :]) & (entry[None, :] < entry[:, None])
-    order = jnp.sum(before.astype(jnp.int32), axis=1, dtype=jnp.int32)
-    place = (holder * GC + order) * FEAT
-    smem = pl.BlockSpec(memory_space=pltpu.SMEM)
-    vmem = pl.BlockSpec(memory_space=pltpu.VMEM)
+    )(ghost_count, arrived, nodes, cand)
     ghost_gap = pl.pallas_call(
-        ghost_kernel,
+        functools.partial(ghost_kernel, blocks=blocks),
         out_shape=jax.ShapeDtypeStruct((1, count), f32),
-        in_specs=[smem, smem, vmem, vmem, vmem],
-        scratch_shapes=[pltpu.VMEM((entries * FEAT, width), f32), pltpu.VMEM((entries, count), f32)],
+        in_specs=[smem, vmem, vmem, vmem],
+        scratch_shapes=[pltpu.VMEM((count, width), f32)],
         name="ghost",
-    )(place, ghost_count, reply, nodes, cand)
+        compiler_params=params,
+    )(ghosts, reply, nodes, left)
     return own_gap.reshape(count), ghost_gap.reshape(count)
 
 

time: 42.4 us -> 35.1 us (0.83)
  blocking collectives: 0 us -> 17.7 us
  waiting for transfers between devices: 10.6 us -> 0.01 us
  starting transfers between devices: 9.96 us -> 2.7 us
  Pallas kernels: 18.1 us -> 11.5 us
  other arithmetic: 0.76 us -> 0 us
    all_to_all x0 -> x1, blocking collectives: none -> 17.7 us  [exchange(): lax.all_to_all(shaped, AXES, split_axis=0, concat_axis=0, tiled=True)]
    all_to_all x2 -> x1, waiting for transfers between devices: 10.6 us -> 0.01 us  [exchange(): lax.all_to_all(shaped, AXES, split_axis=0, concat_axis=0, tiled=True)]
    all_to_all x2 -> x1, starting transfers between devices: 9.96 us -> 2.7 us  [exchange(): lax.all_to_all(shaped, AXES, split_axis=0, concat_axis=0, tiled=True)]
    pallas_call x2, Pallas kernels: 14.1 us -> 10.1 us  [the longest x1 8.2 us: local(): pl.pallas_call(own_kernel, out_shape=(jax.ShapeDtypeStruct((1, count), f3...]
    pallas_call x1, Pallas kernels: 2.13 us -> 0.41 us  [local(): pl.pallas_call(pack_kernel, out_shape=(jax.ShapeDtypeStruct((parts * SEND...]
    pallas_call x1, Pallas kernels: 1.94 us -> 0.93 us  [local(): pl.pallas_call(select_kernel, out_shape=jax.ShapeDtypeStruct((parts * REP...]
    mul x1 -> x0, other arithmetic: 0.56 us -> none  [local(): place = (holder * GC + order) * FEAT]
    unnamed x6 -> x10, local copies, waits for them, and re-layouts: 1.35 us -> 1.66 us
  transfers between devices with their start and end apart: 2 -> 1, of which waited for: 1 -> 0; matrix products, arithmetic and copies ran while one was open for 2% -> 0% of each run, Pallas kernels for 25% -> 23%
where the time goes in v2:
time: 35.1 us; the launch traced here: 34.9 us
  blocking collectives  17.7 us (50%)
  Pallas kernels  11.5 us (33%)
  starting transfers between devices  2.7 us (8%)
  local copies, waits for them, and re-layouts  1.66 us (5%)
  between operations  1.33 us (4%)
    all_to_all x1, blocking collectives, exchange(): lax.all_to_all(shaped, AXES, split_axis=0, concat_axis=0, tiled=True)  17.7 us
    pallas_call x1, Pallas kernels, local(): pl.pallas_call(own_kernel, out_shape=(jax.ShapeDtypeStruct((1, count), f3...  8.2 us
    all_to_all x1, starting transfers between devices, exchange(): lax.all_to_all(shaped, AXES, split_axis=0, concat_axis=0, tiled=True)  2.7 us
    pallas_call x1, Pallas kernels, local(): pl.pallas_call(functools.partial(ghost_kernel, blocks=blocks), out_shape=...  1.92 us
    unnamed x10, local copies, waits for them, and re-layouts  1.66 us
    pallas_call x1, Pallas kernels, local(): pl.pallas_call(select_kernel, out_shape=jax.ShapeDtypeStruct((parts * REP...  0.93 us
  transfers between devices with their start and end apart: 1, of which 0 were waited for; matrix products, arithmetic and copies ran while one was open for 0% of the time, Pallas kernels for 23%

profile of v2, /device:TPU:0, one launch (start us, length us, event | category | flops | bytes accessed | tf_op | source)
XLA Modules:
  0.0 34.9 jit_solution(5828938355190761683)
XLA Ops:
  0.6 0.0 copy-start.3
  0.6 0.0 copy-start.4
  0.6 0.6 %copy-done.3 = s32[1,16]{1,0:T(1,128)S(1)} copy-done((s32[1,16]{1,0:T(1,128)S(1)}, s32[1,16]{1,0:T(1,128)}, u32[]{:S(2)}) %copy-start.3) | copy-done | bytes 88
  1.3 0.0 copy-done.4
  1.3 0.0 copy-start
  1.3 1.0 %copy-done = f32[64,12,128]{2,0,1:T(8,128)S(1)} copy-done((f32[64,12,128]{2,0,1:T(8,128)S(1)}, f32[64,12,128]{2,0,1:T(8,128)}, u32[]{:S(2)}) %copy-start) | copy-done | bytes 393240
  2.3 0.4 %pack.1 = (f32[544,128]{1,0:T(8,128)S(1)}, bf16[192,512]{1,0:T(8,128)(2,1)S(1)}) custom-call(f32[12,64,128]{2,1,0:T(8,128)S(1)} %bitcast.13, s32[1,64]{1,0:T(1,128)S(1)} %bitcast.15, s32[1,16]{1,0:T(1,128)S(1)} %copy-done.3), custom_call_target="tpu_custom_call" | custom-call | tf_op jit(solution)/shard_map/pack/pallas_call | solution.py:211
  2.7 17.7 %all_to_all.10 = f32[32,17,1,128]{3,2,1,0:T(1,128)S(1)} all-to-all(f32[32,17,1,128]{3,2,1,0:T(1,128)S(1)} %bitcast.14), channel_id=1, replica_groups=mesh['gx'=4,'gy'=8] {'gx','gy'}, dimensions={0} | all-to-all | bytes 557056 | tf_op jit(solution)/shard_map/all_to_all | solution.py:198
  20.4 0.9 %select.1 = f32[256,128]{1,0:T(8,128)} custom-call(f32[544,128]{1,0:T(8,128)S(1)} %bitcast.10, bf16[192,512]{1,0:T(8,128)(2,1)S(1)} %get-tuple-element.8.feat_ref), custom_call_target="tpu_custom_call" | custom-call | tf_op jit(solution)/shard_map/select/pallas_call | solution.py:221
  21.4 0.0 copy-start.1
  21.4 0.0 copy-start.2
  21.4 2.7 %all-to-all-start.1 = ((f32[32,8,1,128]{3,1,2,0:T(8,128)}), f32[32,8,1,128]{3,1,2,0:T(8,128)S(1)}, u32[]{:S(2)}, u32[]{:S(2)}) async-start(f32[32,8,1,128]{3,1,2,0:T(8,128)} %bitcast.6), calls=%async_computation.1 | async-start | bytes 262144 | tf_op jit(solution)/shard_map/all_to_all | solution.py:198
  24.7 0.0 copy-done.1
  24.7 0.0 copy-done.2
  24.7 8.2 %own.1 = (f32[1,512]{1,0:T(1,128)}, bf16[512,64]{1,0:T(8,128)(2,1)S(1)}) custom-call(s32[1]{0:T(128)S(6)} %copy.10.limit_ref, f32[544,128]{1,0:T(8,128)S(1)} %bitcast.11, f32[3,512]{1,0:T(4,128)S(1)} %copy-done.1, s32[4,512]{1,0:T(4,128)S(1)} %copy-done.2), custom_call_target="tpu_custom_call" | custom-call | flops 58720256 | bytes 278528 | tf_op jit(solution)/shard_map/own/pallas_call | solution.py:225
  32.9 0.0 all-to-all-done.1
  32.9 1.9 %ghost.1 = f32[1,512]{1,0:T(1,128)} custom-call(s32[1,16]{1,0:T(1,128)S(1)} %copy-done.3, f32[256,128]{1,0:T(8,128)S(1)} %bitcast.12, f32[3,512]{1,0:T(4,128)S(1)} %copy-done.1, bf16[512,64]{1,0:T(8,128)(2,1)S(1)} %get-tuple-element.9.left_ref), custom_call_target="tpu_custom_call" | custom-call | tf_op jit(solution)/shard_map/ghost/pallas_call | solution.py:239
Async XLA Ops:
  0.6 0.7 %copy-start.3 = (s32[1,16]{1,0:T(1,128)S(1)}, s32[1,16]{1,0:T(1,128)}, u32[]{:S(2)}) copy-start(s32[1,16]{1,0:T(1,128)} %wanted_ref.1) | copy-start | bytes 196
  0.6 0.7 %copy-start.4 = (s32[64,1]{0,1:T(1,128)S(1)}, s32[64,1]{0,1:T(1,128)}, u32[]{:S(2)}) copy-start(s32[64,1]{0,1:T(1,128)} %param.7) | copy-start | bytes 772
  1.3 1.0 %copy-start = (f32[64,12,128]{2,0,1:T(8,128)S(1)}, f32[64,12,128]{2,0,1:T(8,128)}, u32[]{:S(2)}) copy-start(f32[64,12,128]{2,0,1:T(8,128)} %param.6) | copy-start | bytes 1179652
  21.4 3.4 %copy-start.1 = (f32[3,512]{1,0:T(4,128)S(1)}, f32[3,512]{1,0:T(4,128)}, u32[]{:S(2)}) copy-start(f32[3,512]{1,0:T(4,128)} %nodes_ref.3) | copy-start | bytes 18436
  21.4 3.4 %copy-start.2 = (s32[4,512]{1,0:T(4,128)S(1)}, s32[4,512]{1,0:T(4,128)}, u32[]{:S(2)}) copy-start(s32[4,512]{1,0:T(4,128)} %cand_ref.1) | copy-start | bytes 24580
  21.4 11.6 %all-to-all-start.1 = ((f32[32,8,1,128]{3,1,2,0:T(8,128)}), f32[32,8,1,128]{3,1,2,0:T(8,128)S(1)}, u32[]{:S(2)}, u32[]{:S(2)}) async-start(f32[32,8,1,128]{3,1,2,0:T(8,128)} %bitcast.6), calls=%async_computation.1 | async-start | bytes 262144 | tf_op jit(solution)/shard_map/all_to_all | solution.py:198

commit v3 on v2

--- a/solution.py
+++ b/solution.py
@@ -13,6 +13,9 @@
 OWN_ROWS = CAP * FEAT
 SEND_ROWS = OWN_ROWS + 1
 REPLY_ROWS = GC * FEAT
+UNROLL = 8
+CHUNK = 64
+GHOST_CHUNKS = 3
 AXES = ("gx", "gy")
 
 far_gap = 10.0
@@ -31,22 +34,19 @@
     return jnp.where(flag, 1.0, 0.0)
 
 
-def pack_kernel(facets_ref, owner_ref, ghosts_ref, out_ref, feat_ref):
+def pack_kernel(facets_hbm, owner_hbm, ghosts_hbm, out_ref, feat_ref, facets_ref, owner_ref, ghosts_ref, sems):
     _, blocks, width = facets_ref.shape
     parts = out_ref.shape[0] // SEND_ROWS
-    ax, ay, az, bx, by, bz, cx, cy, cz, nx, ny, nz = [facets_ref[i] for i in range(12)]
-    third = 1.0 / 3.0
-    squares = lambda u, v, w: u * u + v * v + w * w
-    spread = (squares(ax, bx, cx) + squares(ay, by, cy) + squares(az, bz, cz)) * third
-    offset = spread - (nx * ax + ny * ay + nz * az)
-    feats = [n - (2.0 * third) * (a + b + c) for n, a, b, c in ((nx, ax, bx, cx), (ny, ay, by, cy), (nz, az, bz, cz))]
-    feats.append(offset)
-    splits = [split3(f) for f in feats]
-    table = jnp.concatenate(
-        [jnp.concatenate([splits[c][i] for c in range(FEAT)], axis=1) for i in range(3)], axis=0
-    )
-    feat_ref[...] = table
-
+    fetches = [
+        pltpu.make_async_copy(source, target, sems.at[i])
+        for i, (source, target) in enumerate(
+            ((ghosts_hbm, ghosts_ref), (owner_hbm, owner_ref), (facets_hbm, facets_ref))
+        )
+    ]
+    for fetch in fetches:
+        fetch.start()
+    fetches[0].wait()
+    fetches[1].wait()
     owner_row = owner_ref[...]
     row_id = lax.broadcasted_iota(jnp.int32, (blocks, blocks), 0)
     col_id = lax.broadcasted_iota(jnp.int32, (blocks, blocks), 1)
@@ -57,15 +57,6 @@
     mine = owner_row == part_id
     picks = [to_one(mine & (rank == s)) for s in range(CAP)]
     pick = jnp.concatenate(picks, axis=0).astype(jnp.bfloat16)
-    placed = jnp.dot(jnp.concatenate([pick] * 3, axis=1), table, preferred_element_type=jnp.float32)
-    for s in range(CAP):
-        absent = 1.0 - jnp.sum(picks[s], axis=1, keepdims=True)
-        for c in range(FEAT):
-            piece = placed[s * parts : (s + 1) * parts, c * width : (c + 1) * width]
-            if c == FEAT - 1:
-                piece = piece + penalty * absent
-            out_ref[pl.ds(s * FEAT + c, parts, stride=SEND_ROWS), :] = piece
-
     wanted = ghosts_ref[...]
     entries = wanted.shape[1]
     part_of = lax.broadcasted_iota(jnp.int32, (parts, entries), 0)
@@ -81,6 +72,29 @@
     request = jnp.where(lane == 0, row_first, jnp.where(lane == 1, row_last, 0))
     out_ref[pl.ds(OWN_ROWS, parts, stride=SEND_ROWS), :] = request.astype(jnp.float32)
 
+    fetches[2].wait()
+    ax, ay, az, bx, by, bz, cx, cy, cz, nx, ny, nz = [facets_ref[i] for i in range(12)]
+    third = 1.0 / 3.0
+    squares = lambda u, v, w: u * u + v * v + w * w
+    spread = (squares(ax, bx, cx) + squares(ay, by, cy) + squares(az, bz, cz)) * third
+    offset = spread - (nx * ax + ny * ay + nz * az)
+    feats = [n - (2.0 * third) * (a + b + c) for n, a, b, c in ((nx, ax, bx, cx), (ny, ay, by, cy), (nz, az, bz, cz))]
+    feats.append(offset)
+    splits = [split3(f) for f in feats]
+    table = jnp.concatenate(
+        [jnp.concatenate([splits[c][i] for c in range(FEAT)], axis=1) for i in range(3)], axis=0
+    )
+    feat_ref[...] = table
+
+    placed = jnp.dot(jnp.concatenate([pick] * 3, axis=1), table, preferred_element_type=jnp.float32)
+    for s in range(CAP):
+        absent = 1.0 - jnp.sum(picks[s], axis=1, keepdims=True)
+        for c in range(FEAT):
+            piece = placed[s * parts : (s + 1) * parts, c * width : (c + 1) * width]
+            if c == FEAT - 1:
+                piece = piece + penalty * absent
+            out_ref[pl.ds(s * FEAT + c, parts, stride=SEND_ROWS), :] = piece
+
 
 def select_kernel(arrived_ref, feat_ref, out_ref):
     parts = arrived_ref.shape[0] // SEND_ROWS
@@ -108,27 +122,41 @@
     return [high, middle, low, high, middle, high]
 
 
-def own_kernel(limit_ref, arrived_ref, nodes_ref, cand_ref, out_ref, left_ref, spread_ref, best_ref):
-    parts = arrived_ref.shape[0] // SEND_ROWS
-    width = arrived_ref.shape[1]
+def prep_kernel(limit_ref, wanted_ref, nodes_ref, cand_ref, left_ref, spread_ref, shade_ref, place_ref, *, blocks):
     count = nodes_ref.shape[1]
-    half = count // 2
-    entries = left_ref.shape[1] - 6 * 2 * FEAT
+    _, half, width = spread_ref.shape
+    entries = wanted_ref.shape[1]
+    holder = wanted_ref[...] // blocks
+    row_id = lax.broadcasted_iota(jnp.int32, (entries, entries), 0)
+    col_id = lax.broadcasted_iota(jnp.int32, (entries, entries), 1)
+    holder_col = jnp.sum(jnp.where(row_id == col_id, holder, 0), axis=1, keepdims=True)
+    earlier = (holder_col == holder) & (row_id < col_id)
+    order = jnp.sum(jnp.where(earlier, 1, 0), axis=0, keepdims=True)
+    place_ref[0:1, :] = holder * REPLY_ROWS
+    place_ref[1:2, :] = order
     entry = lax.broadcasted_iota(jnp.int32, (entries, count), 0)
     chosen = entry == cand_ref[0:1, :]
     for k in range(1, cand_ref.shape[0]):
         chosen = chosen | (entry == cand_ref[k : k + 1, :])
     mask = jnp.where(chosen & (entry < limit_ref[0]), 0.0, penalty)
-    left = jnp.concatenate(point_terms(nodes_ref[...]) + [mask], axis=0).T.astype(jnp.bfloat16)
-    left_ref[...] = left
+    left_ref[...] = jnp.concatenate(point_terms(nodes_ref[...]) + [mask], axis=0).T.astype(jnp.bfloat16)
+    shade_ref[...] = mask[:, half:].T
     for c in range(3):
         for g in range(half // width):
             row = nodes_ref[c : c + 1, half + g * width : half + (g + 1) * width]
             spread_ref[c, g * width : (g + 1) * width, :] = jnp.broadcast_to(row, (width, width)).T
+
+
+def own_kernel(arrived_ref, left_ref, spread_ref, out_ref, best_ref):
+    parts = arrived_ref.shape[0] // SEND_ROWS
+    width = arrived_ref.shape[1]
+    count = left_ref.shape[0]
+    half = count // 2
+    entries = left_ref.shape[1] - 6 * 2 * FEAT
     best_ref[...] = jnp.full((count, width), penalty, jnp.float32)
     sublane = lax.broadcasted_iota(jnp.int32, (2 * FEAT, width), 0)
-    chunk = 64
-    unroll = 4
+    chunk = CHUNK
+    unroll = UNROLL
 
     def some_sources(i, carry):
         for u in range(unroll):
@@ -156,40 +184,52 @@
         return carry
 
     lax.fori_loop(0, parts // unroll, some_sources, 0)
-    finish(best_ref, nodes_ref, out_ref)
-
-
-def finish(best_ref, nodes_ref, out_ref, most=None):
-    width = best_ref.shape[1]
-    for g in range(nodes_ref.shape[1] // width):
+    for g in range(count // width):
         here = slice(g * width, (g + 1) * width)
-        least = jnp.min(best_ref[here, :].T, axis=0, keepdims=True)
-        px, py, pz = [nodes_ref[c : c + 1, here] for c in range(3)]
-        gap = least + (px * px + py * py + pz * pz)
-        out_ref[:, here] = gap if most is None else jnp.minimum(most, gap)
-
-
-def ghost_kernel(wanted_ref, reply_ref, nodes_ref, left_ref, out_ref, best_ref, *, blocks):
-    entries = wanted_ref.shape[1]
+        out_ref[:, here] = jnp.min(best_ref[here, :].T, axis=0, keepdims=True)
+
+
+def ghost_kernel(
+    place_ref, reply_ref, nodes_ref, left_ref, spread_ref, shade_ref, own_ref, own_out_ref, out_ref, best_ref
+):
+    entries = place_ref.shape[1]
+    count = nodes_ref.shape[1]
     width = reply_ref.shape[1]
-    holders = [wanted_ref[0, e] // blocks for e in range(entries)]
+    half = spread_ref.shape[1]
+    first = count - GHOST_CHUNKS * CHUNK
+    place = place_ref[...]
     slot = lax.broadcasted_iota(jnp.int32, (2 * FEAT, width), 0) // FEAT
     choice = lax.broadcasted_iota(jnp.int32, (entries, width), 0)
     sides = []
+    starts = []
     for e in range(entries):
-        order = 0
-        for before in range(e):
-            order = order + jnp.where(holders[before] == holders[e], 1, 0)
-        tile = reply_ref[pl.ds(pl.multiple_of(holders[e] * REPLY_ROWS, REPLY_ROWS), REPLY_ROWS), :]
+        start, order = place[0, e], place[1, e]
+        starts.append(start + order * FEAT)
+        tile = reply_ref[pl.ds(pl.multiple_of(start, REPLY_ROWS), REPLY_ROWS), :]
         kept = jnp.where(slot == order, tile, 0.0)
         rows = stack_terms(*split3(kept)) + [to_one(choice == e).astype(jnp.bfloat16)]
         sides.append(jnp.concatenate(rows, axis=0))
-    gaps = jnp.dot(left_ref[...], jnp.concatenate(sides, axis=1), preferred_element_type=jnp.float32)
+    gaps = jnp.dot(left_ref[0:first, :], jnp.concatenate(sides, axis=1), preferred_element_type=jnp.float32)
     least = gaps[:, 0:width]
     for e in range(1, entries):
         least = jnp.minimum(least, gaps[:, e * width : (e + 1) * width])
-    best_ref[...] = least
-    finish(best_ref, nodes_ref, out_ref, far_gap)
+    best_ref[0:first, :] = least
+    for j in range(first, count, CHUNK):
+        here = slice(j - (count - half), j - (count - half) + CHUNK)
+        x, y, z = [spread_ref[c, here, :] for c in range(3)]
+        least = jnp.full((CHUNK, width), penalty, jnp.float32)
+        for e in range(entries):
+            lx, ly, lz, off = [reply_ref[pl.ds(starts[e] + c, 1), :] for c in range(FEAT)]
+            shade = jnp.broadcast_to(shade_ref[here, e : e + 1], (CHUNK, width))
+            least = jnp.minimum(least, ((x * lx + y * ly) + (z * lz + off)) + shade)
+        best_ref[j : j + CHUNK, :] = least
+    px, py, pz = [nodes_ref[c : c + 1, :] for c in range(3)]
+    square = px * px + py * py + pz * pz
+    own_out_ref[...] = own_ref[...] + square
+    for g in range(count // width):
+        here = slice(g * width, (g + 1) * width)
+        least = jnp.min(best_ref[here, :].T, axis=0, keepdims=True)
+        out_ref[:, here] = jnp.minimum(far_gap, least + square[:, here])
 
 
 def exchange(rows, parts):
@@ -208,42 +248,68 @@
     smem = pl.BlockSpec(memory_space=pltpu.SMEM)
     vmem = pl.BlockSpec(memory_space=pltpu.VMEM)
     params = pltpu.CompilerParams(vmem_limit_bytes=16 * 1024 * 1024)
+    hbm = pl.BlockSpec(memory_space=pltpu.HBM)
     outgoing, table = pl.pallas_call(
         pack_kernel,
         out_shape=(
             jax.ShapeDtypeStruct((parts * SEND_ROWS, width), f32),
             jax.ShapeDtypeStruct((3 * blocks, FEAT * width), jnp.bfloat16),
         ),
+        in_specs=[hbm] * 3,
+        out_specs=(vmem, vmem),
+        scratch_shapes=[
+            pltpu.VMEM((12, blocks, width), f32),
+            pltpu.VMEM((1, blocks), jnp.int32),
+            pltpu.VMEM((1, entries), jnp.int32),
+            pltpu.SemaphoreType.DMA((3,)),
+        ],
         name="pack",
         compiler_params=params,
-    )(jnp.transpose(facets, (1, 0, 2)), owner.T, ghosts)
+    )(*[pltpu.with_memory_space_constraint(v, pltpu.HBM) for v in (jnp.transpose(facets, (1, 0, 2)), owner.T, ghosts)])
     arrived = exchange(outgoing, parts)
+    left, spread, shade, place = pl.pallas_call(
+        functools.partial(prep_kernel, blocks=blocks),
+        out_shape=(
+            jax.ShapeDtypeStruct((count, 6 * 2 * FEAT + entries), jnp.bfloat16),
+            jax.ShapeDtypeStruct((3, count // 2, width), f32),
+            jax.ShapeDtypeStruct((count // 2, entries), f32),
+            jax.ShapeDtypeStruct((2, entries), jnp.int32),
+        ),
+        in_specs=[smem, vmem, vmem, vmem],
+        out_specs=(vmem, vmem, vmem, vmem),
+        name="prep",
+        compiler_params=params,
+    )(ghost_count, ghosts, nodes, cand)
     answer = pl.pallas_call(
-        select_kernel, out_shape=jax.ShapeDtypeStruct((parts * REPLY_ROWS, width), f32), name="select", compiler_params=params
+        select_kernel,
+        out_shape=jax.ShapeDtypeStruct((parts * REPLY_ROWS, width), f32),
+        in_specs=[vmem, vmem],
+        out_specs=vmem,
+        name="select",
+        compiler_params=params,
     )(arrived, table)
     reply = exchange(answer, parts)
-    own_gap, left = pl.pallas_call(
+    own_least = pl.pallas_call(
         own_kernel,
-        out_shape=(
-            jax.ShapeDtypeStruct((1, count), f32),
-            jax.ShapeDtypeStruct((count, 6 * 2 * FEAT + entries), jnp.bfloat16),
-        ),
-        in_specs=[smem, vmem, vmem, vmem],
-        scratch_shapes=[pltpu.VMEM((3, count // 2, width), f32), pltpu.VMEM((count, width), f32)],
+        out_shape=jax.ShapeDtypeStruct((1, count), f32),
+        in_specs=[vmem] * 3,
+        out_specs=vmem,
+        scratch_shapes=[pltpu.VMEM((count, width), f32)],
         name="own",
         compiler_params=params,
         cost_estimate=pl.CostEstimate(
             flops=7 * parts * CAP * width * count, bytes_accessed=parts * SEND_ROWS * width * 4, transcendentals=0
         ),
-    )(ghost_count, arrived, nodes, cand)
-    ghost_gap = pl.pallas_call(
-        functools.partial(ghost_kernel, blocks=blocks),
-        out_shape=jax.ShapeDtypeStruct((1, count), f32),
-        in_specs=[smem, vmem, vmem, vmem],
+    )(arrived, left, spread)
+    own_gap, ghost_gap = pl.pallas_call(
+        ghost_kernel,
+        out_shape=[jax.ShapeDtypeStruct((1, count), f32)] * 2,
+        in_specs=[vmem] * 7,
+        out_specs=[vmem, vmem],
         scratch_shapes=[pltpu.VMEM((count, width), f32)],
         name="ghost",
         compiler_params=params,
-    )(ghosts, reply, nodes, left)
+    )(place, reply, nodes, left, spread, shade, own_least)
     return own_gap.reshape(count), ghost_gap.reshape(count)
 
 

time: 35.1 us -> 33.2 us (0.946)
  local copies, waits for them, and re-layouts: 1.66 us -> 0.01 us
  Pallas kernels: 11.5 us -> 10.8 us
    unnamed x10 -> x6, local copies, waits for them, and re-layouts: 1.66 us -> 0.01 us
    pallas_call x2 -> x3, Pallas kernels: 10.1 us -> 8.58 us  [the longest x1 6.81 us: local(): pl.pallas_call(own_kernel, out_shape=jax.ShapeDtypeStruct((1, count), f32...]
    pallas_call x1, Pallas kernels: 0.41 us -> 1.29 us  [local(): pl.pallas_call(pack_kernel, out_shape=(jax.ShapeDtypeStruct((parts * SEND...]
    all_to_all x1, waiting for transfers between devices: 0.01 us -> 0.36 us  [exchange(): lax.all_to_all(shaped, AXES, split_axis=0, concat_axis=0, tiled=True)]
  transfers between devices with their start and end apart: 1 -> 1, of which waited for: 0 -> 1; matrix products, arithmetic and copies ran while one was open for 0% -> 0% of each run, Pallas kernels for 23% -> 22%
where the time goes in v3:
time: 33.2 us; the launch traced here: 32.9 us
  blocking collectives  17.7 us (53%)
  Pallas kernels  10.8 us (33%)
  starting transfers between devices  2.69 us (8%)
  between operations  1.35 us (4%)
  waiting for transfers between devices  0.36 us (1%)
    all_to_all x1, blocking collectives, exchange(): lax.all_to_all(shaped, AXES, split_axis=0, concat_axis=0, tiled=True)  17.7 us
    pallas_call x1, Pallas kernels, local(): pl.pallas_call(own_kernel, out_shape=jax.ShapeDtypeStruct((1, count), f32...  6.81 us
    all_to_all x1, starting transfers between devices, exchange(): lax.all_to_all(shaped, AXES, split_axis=0, concat_axis=0, tiled=True)  2.69 us
    pallas_call x1, Pallas kernels, local(): pl.pallas_call(ghost_kernel, out_shape=[jax.ShapeDtypeStruct((1, count),...  1.5 us
    pallas_call x1, Pallas kernels, local(): pl.pallas_call(pack_kernel, out_shape=(jax.ShapeDtypeStruct((parts * SEND...  1.29 us
    pallas_call x1, Pallas kernels, local(): pl.pallas_call(select_kernel, out_shape=jax.ShapeDtypeStruct((parts * REP...  0.93 us
  transfers between devices with their start and end apart: 1, of which 1 were waited for; matrix products, arithmetic and copies ran while one was open for 0% of the time, Pallas kernels for 22%

profile of v3, /device:TPU:0, one launch (start us, length us, event | category | flops | bytes accessed | tf_op | source)
XLA Modules:
  0.0 32.9 jit_solution(14872595393831241630)
XLA Ops:
  0.6 1.3 %pack.1 = (f32[544,128]{1,0:T(8,128)S(1)}, bf16[192,512]{1,0:T(8,128)(2,1)S(1)}) custom-call(f32[12,64,128]{2,1,0:T(8,128)} %bitcast.14, s32[1,64]{1,0:T(1,128)} %bitcast.15, s32[1,16]{1,0:T(1,128)} %ghosts_hbm.1), custom_call_target="tpu_custom_call" | custom-call | tf_op jit(solution)/shard_map/pack/pallas_call | solution.py:252
  1.9 17.7 %all_to_all.10 = f32[32,17,1,128]{3,2,1,0:T(1,128)S(1)} all-to-all(f32[32,17,1,128]{3,2,1,0:T(1,128)S(1)} %bitcast.13), channel_id=1, replica_groups=mesh['gx'=4,'gy'=8] {'gx','gy'}, dimensions={0} | all-to-all | bytes 557056 | tf_op jit(solution)/shard_map/all_to_all | solution.py:238
  19.7 0.9 %select.1 = f32[256,128]{1,0:T(8,128)} custom-call(f32[544,128]{1,0:T(8,128)S(1)} %bitcast.10, bf16[192,512]{1,0:T(8,128)(2,1)S(1)} %get-tuple-element.12.feat_ref), custom_call_target="tpu_custom_call" | custom-call | tf_op jit(solution)/shard_map/select/pallas_call | solution.py:283
  20.6 0.0 copy-start
  20.6 0.0 copy-start.1
  20.6 2.7 %all-to-all-start.1 = ((f32[32,8,1,128]{3,1,2,0:T(8,128)}), f32[32,8,1,128]{3,1,2,0:T(8,128)S(1)}, u32[]{:S(2)}, u32[]{:S(2)}) async-start(f32[32,8,1,128]{3,1,2,0:T(8,128)} %bitcast.5), calls=%async_computation.1 | async-start | bytes 262144 | tf_op jit(solution)/shard_map/all_to_all | solution.py:238
  23.3 0.0 copy-start.2
  24.0 0.0 copy-done
  24.0 0.0 copy-done.1
  24.0 0.0 copy-done.2
  24.0 0.3 prep.1
  24.3 6.8 %own.1.own_ref = f32[1,512]{1,0:T(1,128)S(1)} custom-call(f32[544,128]{1,0:T(8,128)S(1)} %bitcast.11, bf16[512,64]{1,0:T(8,128)(2,1)S(1)} %get-tuple-element.13.left_ref, f32[3,256,128]{2,1,0:T(8,128)S(1)} %get-tuple-element.14.spread_ref), custom_call_target="tpu_custom_call" | custom-call | flops 58720256 | bytes 278528 | tf_op jit(solution)/shard_map/own/pallas_call | solution.py:292
  31.1 0.4 %all-to-all-done.1 = f32[32,8,1,128]{3,1,2,0:T(8,128)S(1)} async-done(((f32[32,8,1,128]{3,1,2,0:T(8,128)}), f32[32,8,1,128]{3,1,2,0:T(8,128)S(1)}, u32[]{:S(2)}, u32[]{:S(2)}) %all-to-all-start.1) | async-done | bytes 131104 | tf_op jit(solution)/shard_map/all_to_all | solution.py:238
  31.4 1.5 %ghost.1 = (f32[1,512]{1,0:T(1,128)}, f32[1,512]{1,0:T(1,128)}) custom-call(s32[2,16]{1,0:T(2,128)S(1)} %get-tuple-element.10.place_ref, f32[256,128]{1,0:T(8,128)S(1)} %bitcast.12, f32[3,512]{1,0:T(4,128)S(1)} %copy-done, bf16[512,64]{1,0:T(8,128)(2,1)S(1)} %get-tuple-element.13.left_ref, f32[3,256,128]{2,1,0:T(8,128)S(1)} %get-tuple-element.14.spread_ref, ...), custom_call_target="tpu_custom_call" | custom-call | tf_op jit(solution)/shard_map/ghost/pallas_call | solution.py:304
Async XLA Ops:
  20.6 3.4 %copy-start = (f32[3,512]{1,0:T(4,128)S(1)}, f32[3,512]{1,0:T(4,128)}, u32[]{:S(2)}) copy-start(f32[3,512]{1,0:T(4,128)} %nodes_ref.3) | copy-start | bytes 18436
  20.6 3.4 %copy-start.1 = (s32[4,512]{1,0:T(4,128)S(1)}, s32[4,512]{1,0:T(4,128)}, u32[]{:S(2)}) copy-start(s32[4,512]{1,0:T(4,128)} %cand_ref.1) | copy-start | bytes 24580
  20.6 10.9 %all-to-all-start.1 = ((f32[32,8,1,128]{3,1,2,0:T(8,128)}), f32[32,8,1,128]{3,1,2,0:T(8,128)S(1)}, u32[]{:S(2)}, u32[]{:S(2)}) async-start(f32[32,8,1,128]{3,1,2,0:T(8,128)} %bitcast.5), calls=%async_computation.1 | async-start | bytes 262144 | tf_op jit(solution)/shard_map/all_to_all | solution.py:238
  23.3 0.7 %copy-start.2 = (s32[1,16]{1,0:T(1,128)S(1)}, s32[1,16]{1,0:T(1,128)}, u32[]{:S(2)}) copy-start(s32[1,16]{1,0:T(1,128)} %ghosts_hbm.1) | copy-start | bytes 196

commit v4 on v3

--- a/solution.py
+++ b/solution.py
@@ -15,7 +15,8 @@
 REPLY_ROWS = GC * FEAT
 UNROLL = 8
 CHUNK = 64
-GHOST_CHUNKS = 3
+GHOST_CHUNKS = 2
+GHOST_GROUP = 8
 AXES = ("gx", "gy")
 
 far_gap = 10.0
@@ -34,7 +35,7 @@
     return jnp.where(flag, 1.0, 0.0)
 
 
-def pack_kernel(facets_hbm, owner_hbm, ghosts_hbm, out_ref, feat_ref, facets_ref, owner_ref, ghosts_ref, sems):
+def pack_kernel(facets_hbm, owner_hbm, ghosts_hbm, out_ref, table_ref, facets_ref, owner_ref, ghosts_ref, sems):
     _, blocks, width = facets_ref.shape
     parts = out_ref.shape[0] // SEND_ROWS
     fetches = [
@@ -53,10 +54,12 @@
     owner_col = jnp.sum(jnp.where(row_id == col_id, owner_row, 0), axis=1, keepdims=True)
     earlier = (owner_col == owner_row) & (row_id < col_id)
     rank = jnp.sum(jnp.where(earlier, 1, 0), axis=0, keepdims=True)
-    part_id = lax.broadcasted_iota(jnp.int32, (parts, blocks), 0)
-    mine = owner_row == part_id
-    picks = [to_one(mine & (rank == s)) for s in range(CAP)]
-    pick = jnp.concatenate(picks, axis=0).astype(jnp.bfloat16)
+    places = owner_row * SEND_ROWS + rank * FEAT
+    starts = [places[0, b] for b in range(blocks)]
+    out_ref[...] = jnp.zeros(out_ref.shape, jnp.float32)
+    for slot in range(CAP):
+        out_ref[pl.ds(slot * FEAT + FEAT - 1, parts, stride=SEND_ROWS), :] = jnp.full((parts, width), penalty, jnp.float32)
+
     wanted = ghosts_ref[...]
     entries = wanted.shape[1]
     part_of = lax.broadcasted_iota(jnp.int32, (parts, entries), 0)
@@ -80,36 +83,19 @@
     offset = spread - (nx * ax + ny * ay + nz * az)
     feats = [n - (2.0 * third) * (a + b + c) for n, a, b, c in ((nx, ax, bx, cx), (ny, ay, by, cy), (nz, az, bz, cz))]
     feats.append(offset)
-    splits = [split3(f) for f in feats]
-    table = jnp.concatenate(
-        [jnp.concatenate([splits[c][i] for c in range(FEAT)], axis=1) for i in range(3)], axis=0
-    )
-    feat_ref[...] = table
-
-    placed = jnp.dot(jnp.concatenate([pick] * 3, axis=1), table, preferred_element_type=jnp.float32)
-    for s in range(CAP):
-        absent = 1.0 - jnp.sum(picks[s], axis=1, keepdims=True)
-        for c in range(FEAT):
-            piece = placed[s * parts : (s + 1) * parts, c * width : (c + 1) * width]
-            if c == FEAT - 1:
-                piece = piece + penalty * absent
-            out_ref[pl.ds(s * FEAT + c, parts, stride=SEND_ROWS), :] = piece
-
-
-def select_kernel(arrived_ref, feat_ref, out_ref):
+    for c in range(FEAT):
+        table_ref[pl.ds(c, blocks, stride=FEAT), :] = feats[c]
+    for b in range(blocks):
+        out_ref[pl.ds(starts[b], FEAT), :] = table_ref[b * FEAT : (b + 1) * FEAT, :]
+
+
+def select_kernel(arrived_ref, table_ref, out_ref):
     parts = arrived_ref.shape[0] // SEND_ROWS
-    width = arrived_ref.shape[1]
-    blocks = feat_ref.shape[0] // 3
-    request = arrived_ref[pl.ds(OWN_ROWS, parts, stride=SEND_ROWS), :].astype(jnp.int32)
-    block_id = lax.broadcasted_iota(jnp.int32, (parts, blocks), 1)
-    pick = jnp.concatenate([to_one(request[:, s : s + 1] == block_id) for s in range(GC)], axis=0)
-    pick = pick.astype(jnp.bfloat16)
-    rows = jnp.dot(jnp.concatenate([pick] * 3, axis=1), feat_ref[...], preferred_element_type=jnp.float32)
-    for s in range(GC):
-        for c in range(FEAT):
-            out_ref[pl.ds(s * FEAT + c, parts, stride=REPLY_ROWS), :] = rows[
-                s * parts : (s + 1) * parts, c * width : (c + 1) * width
-            ]
+    request = arrived_ref[pl.ds(OWN_ROWS, parts, stride=SEND_ROWS), :].astype(jnp.int32) * FEAT
+    for d in range(parts):
+        for s in range(GC):
+            row = d * REPLY_ROWS + s * FEAT
+            out_ref[row : row + FEAT, :] = table_ref[pl.ds(pl.multiple_of(request[d, s], FEAT), FEAT), :]
 
 
 def stack_terms(high, middle, low):
@@ -190,7 +176,7 @@
 
 
 def ghost_kernel(
-    place_ref, reply_ref, nodes_ref, left_ref, spread_ref, shade_ref, own_ref, own_out_ref, out_ref, best_ref
+    limit_ref, place_ref, reply_ref, nodes_ref, left_ref, spread_ref, shade_ref, own_ref, own_out_ref, out_ref, best_ref
 ):
     entries = place_ref.shape[1]
     count = nodes_ref.shape[1]
@@ -200,29 +186,38 @@
     place = place_ref[...]
     slot = lax.broadcasted_iota(jnp.int32, (2 * FEAT, width), 0) // FEAT
     choice = lax.broadcasted_iota(jnp.int32, (entries, width), 0)
-    sides = []
-    starts = []
-    for e in range(entries):
-        start, order = place[0, e], place[1, e]
-        starts.append(start + order * FEAT)
-        tile = reply_ref[pl.ds(pl.multiple_of(start, REPLY_ROWS), REPLY_ROWS), :]
-        kept = jnp.where(slot == order, tile, 0.0)
-        rows = stack_terms(*split3(kept)) + [to_one(choice == e).astype(jnp.bfloat16)]
-        sides.append(jnp.concatenate(rows, axis=0))
-    gaps = jnp.dot(left_ref[0:first, :], jnp.concatenate(sides, axis=1), preferred_element_type=jnp.float32)
-    least = gaps[:, 0:width]
-    for e in range(1, entries):
-        least = jnp.minimum(least, gaps[:, e * width : (e + 1) * width])
-    best_ref[0:first, :] = least
-    for j in range(first, count, CHUNK):
-        here = slice(j - (count - half), j - (count - half) + CHUNK)
-        x, y, z = [spread_ref[c, here, :] for c in range(3)]
-        least = jnp.full((CHUNK, width), penalty, jnp.float32)
-        for e in range(entries):
-            lx, ly, lz, off = [reply_ref[pl.ds(starts[e] + c, 1), :] for c in range(FEAT)]
-            shade = jnp.broadcast_to(shade_ref[here, e : e + 1], (CHUNK, width))
-            least = jnp.minimum(least, ((x * lx + y * ly) + (z * lz + off)) + shade)
-        best_ref[j : j + CHUNK, :] = least
+    best_ref[...] = jnp.full((count, width), penalty, jnp.float32)
+    def some_entries(members):
+        sides = []
+        starts = []
+        for e in members:
+            start, order = place[0, e], place[1, e]
+            starts.append(start + order * FEAT)
+            tile = reply_ref[pl.ds(pl.multiple_of(start, REPLY_ROWS), REPLY_ROWS), :]
+            kept = jnp.where(slot == order, tile, 0.0)
+            rows = stack_terms(*split3(kept)) + [to_one(choice == e).astype(jnp.bfloat16)]
+            sides.append(jnp.concatenate(rows, axis=0))
+        gaps = jnp.dot(left_ref[0:first, :], jnp.concatenate(sides, axis=1), preferred_element_type=jnp.float32)
+        least = best_ref[0:first, :]
+        for i in range(len(sides)):
+            least = jnp.minimum(least, gaps[:, i * width : (i + 1) * width])
+        best_ref[0:first, :] = least
+        for j in range(first, count, CHUNK):
+            here = slice(j - (count - half), j - (count - half) + CHUNK)
+            x, y, z = [spread_ref[c, here, :] for c in range(3)]
+            least = best_ref[j : j + CHUNK, :]
+            for e, start in zip(members, starts):
+                lx, ly, lz, off = [reply_ref[pl.ds(start + c, 1), :] for c in range(FEAT)]
+                shade = jnp.broadcast_to(shade_ref[here, e : e + 1], (CHUNK, width))
+                least = jnp.minimum(least, ((x * lx + y * ly) + (z * lz + off)) + shade)
+            best_ref[j : j + CHUNK, :] = least
+
+    for group in range(0, entries, GHOST_GROUP):
+        members = range(group, min(group + GHOST_GROUP, entries))
+        if group == 0:
+            some_entries(members)
+        else:
+            pl.when(limit_ref[0] > group)(functools.partial(some_entries, members))
     px, py, pz = [nodes_ref[c : c + 1, :] for c in range(3)]
     square = px * px + py * py + pz * pz
     own_out_ref[...] = own_ref[...] + square
@@ -253,7 +248,7 @@
         pack_kernel,
         out_shape=(
             jax.ShapeDtypeStruct((parts * SEND_ROWS, width), f32),
-            jax.ShapeDtypeStruct((3 * blocks, FEAT * width), jnp.bfloat16),
+            jax.ShapeDtypeStruct((blocks * FEAT, width), f32),
         ),
         in_specs=[hbm] * 3,
         out_specs=(vmem, vmem),
@@ -304,12 +299,12 @@
     own_gap, ghost_gap = pl.pallas_call(
         ghost_kernel,
         out_shape=[jax.ShapeDtypeStruct((1, count), f32)] * 2,
-        in_specs=[vmem] * 7,
+        in_specs=[smem] + [vmem] * 7,
         out_specs=[vmem, vmem],
         scratch_shapes=[pltpu.VMEM((count, width), f32)],
         name="ghost",
         compiler_params=params,
-    )(place, reply, nodes, left, spread, shade, own_least)
+    )(ghost_count, place, reply, nodes, left, spread, shade, own_least)
     return own_gap.reshape(count), ghost_gap.reshape(count)
 
 

time: 33.2 us -> 33.1 us (level)
  no operation moved by 1% of the time
where the time goes in v4:
time: 33.1 us; the launch traced here: 32.9 us
  blocking collectives  17.7 us (53%)
  Pallas kernels  10.7 us (32%)
  starting transfers between devices  2.69 us (8%)
  between operations  1.35 us (4%)
  waiting for transfers between devices  0.36 us (1%)
    all_to_all x1, blocking collectives, exchange(): lax.all_to_all(shaped, AXES, split_axis=0, concat_axis=0, tiled=True)  17.7 us
    pallas_call x1, Pallas kernels, local(): pl.pallas_call(own_kernel, out_shape=jax.ShapeDtypeStruct((1, count), f32...  6.81 us
    all_to_all x1, starting transfers between devices, exchange(): lax.all_to_all(shaped, AXES, split_axis=0, concat_axis=0, tiled=True)  2.69 us
    pallas_call x1, Pallas kernels, local(): pl.pallas_call(ghost_kernel, out_shape=[jax.ShapeDtypeStruct((1, count),...  1.72 us
    pallas_call x1, Pallas kernels, local(): pl.pallas_call(pack_kernel, out_shape=(jax.ShapeDtypeStruct((parts * SEND...  1.14 us
    pallas_call x1, Pallas kernels, local(): pl.pallas_call(select_kernel, out_shape=jax.ShapeDtypeStruct((parts * REP...  0.8 us
  transfers between devices with their start and end apart: 1, of which 1 were waited for; matrix products, arithmetic and copies ran while one was open for 0% of the time, Pallas kernels for 22%

profile of v4, /device:TPU:0, one launch (start us, length us, event | category | flops | bytes accessed | tf_op | source)
XLA Modules:
  0.0 32.9 jit_solution(17647591772117687145)
XLA Ops:
  0.6 1.1 %pack.1 = (f32[544,128]{1,0:T(8,128)S(1)}, f32[256,128]{1,0:T(8,128)S(1)}) custom-call(f32[12,64,128]{2,1,0:T(8,128)} %bitcast.14, s32[1,64]{1,0:T(1,128)} %bitcast.15, s32[1,16]{1,0:T(1,128)} %ghosts_hbm.1), custom_call_target="tpu_custom_call" | custom-call | tf_op jit(solution)/shard_map/pack/pallas_call | solution.py:247
  1.8 17.7 %all_to_all.10 = f32[32,17,1,128]{3,2,1,0:T(1,128)S(1)} all-to-all(f32[32,17,1,128]{3,2,1,0:T(1,128)S(1)} %bitcast.13), channel_id=1, replica_groups=mesh['gx'=4,'gy'=8] {'gx','gy'}, dimensions={0} | all-to-all | bytes 557056 | tf_op jit(solution)/shard_map/all_to_all | solution.py:233
  19.5 0.8 %select.1 = f32[256,128]{1,0:T(8,128)} custom-call(f32[544,128]{1,0:T(8,128)S(1)} %bitcast.10, f32[256,128]{1,0:T(8,128)S(1)} %get-tuple-element.12.table_ref), custom_call_target="tpu_custom_call" | custom-call | tf_op jit(solution)/shard_map/select/pallas_call | solution.py:278
  20.3 0.0 copy-start
  20.3 0.0 copy-start.1
  20.3 2.7 %all-to-all-start.1 = ((f32[32,8,1,128]{3,1,2,0:T(8,128)}), f32[32,8,1,128]{3,1,2,0:T(8,128)S(1)}, u32[]{:S(2)}, u32[]{:S(2)}) async-start(f32[32,8,1,128]{3,1,2,0:T(8,128)} %bitcast.5), calls=%async_computation.1 | async-start | bytes 262144 | tf_op jit(solution)/shard_map/all_to_all | solution.py:233
  23.0 0.0 copy-start.2
  23.7 0.0 copy-done
  23.7 0.0 copy-done.1
  23.7 0.0 copy-done.2
  23.7 0.3 prep.1
  24.0 6.8 %own.1.own_ref = f32[1,512]{1,0:T(1,128)S(1)} custom-call(f32[544,128]{1,0:T(8,128)S(1)} %bitcast.11, bf16[512,64]{1,0:T(8,128)(2,1)S(1)} %get-tuple-element.13.left_ref, f32[3,256,128]{2,1,0:T(8,128)S(1)} %get-tuple-element.14.spread_ref), custom_call_target="tpu_custom_call" | custom-call | flops 58720256 | bytes 278528 | tf_op jit(solution)/shard_map/own/pallas_call | solution.py:287
  30.8 0.4 %all-to-all-done.1 = f32[32,8,1,128]{3,1,2,0:T(8,128)S(1)} async-done(((f32[32,8,1,128]{3,1,2,0:T(8,128)}), f32[32,8,1,128]{3,1,2,0:T(8,128)S(1)}, u32[]{:S(2)}, u32[]{:S(2)}) %all-to-all-start.1) | async-done | bytes 131104 | tf_op jit(solution)/shard_map/all_to_all | solution.py:233
  31.2 1.7 %ghost.1 = (f32[1,512]{1,0:T(1,128)}, f32[1,512]{1,0:T(1,128)}) custom-call(s32[1]{0:T(128)S(6)} %copy.10.limit_ref, s32[2,16]{1,0:T(2,128)S(1)} %get-tuple-element.10.place_ref, f32[256,128]{1,0:T(8,128)S(1)} %bitcast.12, f32[3,512]{1,0:T(4,128)S(1)} %copy-done, bf16[512,64]{1,0:T(8,128)(2,1)S(1)} %get-tuple-element.13.left_ref, ...), custom_call_target="tpu_custom_call" | custom-call | tf_op jit(solution)/shard_map/ghost/pallas_call | solution.py:299
Async XLA Ops:
  20.3 3.4 %copy-start = (f32[3,512]{1,0:T(4,128)S(1)}, f32[3,512]{1,0:T(4,128)}, u32[]{:S(2)}) copy-start(f32[3,512]{1,0:T(4,128)} %nodes_ref.3) | copy-start | bytes 18436
  20.3 3.4 %copy-start.1 = (s32[4,512]{1,0:T(4,128)S(1)}, s32[4,512]{1,0:T(4,128)}, u32[]{:S(2)}) copy-start(s32[4,512]{1,0:T(4,128)} %cand_ref.1) | copy-start | bytes 24580
  20.3 10.9 %all-to-all-start.1 = ((f32[32,8,1,128]{3,1,2,0:T(8,128)}), f32[32,8,1,128]{3,1,2,0:T(8,128)S(1)}, u32[]{:S(2)}, u32[]{:S(2)}) async-start(f32[32,8,1,128]{3,1,2,0:T(8,128)} %bitcast.5), calls=%async_computation.1 | async-start | bytes 262144 | tf_op jit(solution)/shard_map/all_to_all | solution.py:233
  23.0 0.7 %copy-start.2 = (s32[1,16]{1,0:T(1,128)S(1)}, s32[1,16]{1,0:T(1,128)}, u32[]{:S(2)}) copy-start(s32[1,16]{1,0:T(1,128)} %ghosts_hbm.1) | copy-start | bytes 196

commit v5 on v4

--- a/solution.py
+++ b/solution.py
@@ -16,7 +16,8 @@
 UNROLL = 8
 CHUNK = 64
 GHOST_CHUNKS = 2
-GHOST_GROUP = 8
+SPREAD = 128
+GHOST_LEVELS = (4, 8, 1 << 30)
 AXES = ("gx", "gy")
 
 far_gap = 10.0
@@ -110,7 +111,8 @@
 
 def prep_kernel(limit_ref, wanted_ref, nodes_ref, cand_ref, left_ref, spread_ref, shade_ref, place_ref, *, blocks):
     count = nodes_ref.shape[1]
-    _, half, width = spread_ref.shape
+    _, spread_count, width = spread_ref.shape
+    start = count - spread_count
     entries = wanted_ref.shape[1]
     holder = wanted_ref[...] // blocks
     row_id = lax.broadcasted_iota(jnp.int32, (entries, entries), 0)
@@ -126,10 +128,10 @@
         chosen = chosen | (entry == cand_ref[k : k + 1, :])
     mask = jnp.where(chosen & (entry < limit_ref[0]), 0.0, penalty)
     left_ref[...] = jnp.concatenate(point_terms(nodes_ref[...]) + [mask], axis=0).T.astype(jnp.bfloat16)
-    shade_ref[...] = mask[:, half:].T
+    shade_ref[...] = mask[:, start:].T
     for c in range(3):
-        for g in range(half // width):
-            row = nodes_ref[c : c + 1, half + g * width : half + (g + 1) * width]
+        for g in range(spread_count // width):
+            row = nodes_ref[c : c + 1, start + g * width : start + (g + 1) * width]
             spread_ref[c, g * width : (g + 1) * width, :] = jnp.broadcast_to(row, (width, width)).T
 
 
@@ -137,7 +139,7 @@
     parts = arrived_ref.shape[0] // SEND_ROWS
     width = arrived_ref.shape[1]
     count = left_ref.shape[0]
-    half = count // 2
+    first = count - spread_ref.shape[1]
     entries = left_ref.shape[1] - 6 * 2 * FEAT
     best_ref[...] = jnp.full((count, width), penalty, jnp.float32)
     sublane = lax.broadcasted_iota(jnp.int32, (2 * FEAT, width), 0)
@@ -154,14 +156,14 @@
                     kept = jnp.where((sublane >= FEAT) == (part == 1), tile, 0.0)
                     rows = stack_terms(*split3(kept)) + [jnp.zeros((entries, width), jnp.bfloat16)]
                     sides.append(jnp.concatenate(rows, axis=0))
-            gaps = jnp.dot(left_ref[0:half, :], jnp.concatenate(sides, axis=1), preferred_element_type=jnp.float32)
-            least = best_ref[0:half, :]
+            gaps = jnp.dot(left_ref[0:first, :], jnp.concatenate(sides, axis=1), preferred_element_type=jnp.float32)
+            least = best_ref[0:first, :]
             for s in range(CAP):
                 least = jnp.minimum(least, gaps[:, s * width : (s + 1) * width])
-            best_ref[0:half, :] = least
-            for j in range(half // chunk):
+            best_ref[0:first, :] = least
+            for j in range((count - first) // chunk):
                 x, y, z = [spread_ref[c, j * chunk : (j + 1) * chunk, :] for c in range(3)]
-                here = slice(half + j * chunk, half + (j + 1) * chunk)
+                here = slice(first + j * chunk, first + (j + 1) * chunk)
                 least = best_ref[here, :]
                 for s in range(CAP):
                     lx, ly, lz, off = [arrived_ref[pl.ds(base + s * FEAT + c, 1), :] for c in range(FEAT)]
@@ -181,12 +183,12 @@
     entries = place_ref.shape[1]
     count = nodes_ref.shape[1]
     width = reply_ref.shape[1]
-    half = spread_ref.shape[1]
+    spread_start = count - spread_ref.shape[1]
     first = count - GHOST_CHUNKS * CHUNK
     place = place_ref[...]
     slot = lax.broadcasted_iota(jnp.int32, (2 * FEAT, width), 0) // FEAT
     choice = lax.broadcasted_iota(jnp.int32, (entries, width), 0)
-    best_ref[...] = jnp.full((count, width), penalty, jnp.float32)
+
     def some_entries(members):
         sides = []
         starts = []
@@ -198,26 +200,26 @@
             rows = stack_terms(*split3(kept)) + [to_one(choice == e).astype(jnp.bfloat16)]
             sides.append(jnp.concatenate(rows, axis=0))
         gaps = jnp.dot(left_ref[0:first, :], jnp.concatenate(sides, axis=1), preferred_element_type=jnp.float32)
-        least = best_ref[0:first, :]
-        for i in range(len(sides)):
-            least = jnp.minimum(least, gaps[:, i * width : (i + 1) * width])
-        best_ref[0:first, :] = least
+        best_ref[0:first, :] = functools.reduce(
+            jnp.minimum, [gaps[:, i * width : (i + 1) * width] for i in range(len(sides))]
+        )
         for j in range(first, count, CHUNK):
-            here = slice(j - (count - half), j - (count - half) + CHUNK)
+            here = slice(j - spread_start, j - spread_start + CHUNK)
             x, y, z = [spread_ref[c, here, :] for c in range(3)]
-            least = best_ref[j : j + CHUNK, :]
+            least = jnp.full((CHUNK, width), penalty, jnp.float32)
             for e, start in zip(members, starts):
                 lx, ly, lz, off = [reply_ref[pl.ds(start + c, 1), :] for c in range(FEAT)]
                 shade = jnp.broadcast_to(shade_ref[here, e : e + 1], (CHUNK, width))
                 least = jnp.minimum(least, ((x * lx + y * ly) + (z * lz + off)) + shade)
             best_ref[j : j + CHUNK, :] = least
 
-    for group in range(0, entries, GHOST_GROUP):
-        members = range(group, min(group + GHOST_GROUP, entries))
-        if group == 0:
-            some_entries(members)
-        else:
-            pl.when(limit_ref[0] > group)(functools.partial(some_entries, members))
+    least = 0
+    for most in GHOST_LEVELS:
+        some = min(most, entries)
+        if some > least:
+            enough = limit_ref[0] > least if some == entries else (limit_ref[0] > least) & (limit_ref[0] <= some)
+            pl.when(enough)(functools.partial(some_entries, range(some)))
+        least = some
     px, py, pz = [nodes_ref[c : c + 1, :] for c in range(3)]
     square = px * px + py * py + pz * pz
     own_out_ref[...] = own_ref[...] + square
@@ -266,8 +268,8 @@
         functools.partial(prep_kernel, blocks=blocks),
         out_shape=(
             jax.ShapeDtypeStruct((count, 6 * 2 * FEAT + entries), jnp.bfloat16),
-            jax.ShapeDtypeStruct((3, count // 2, width), f32),
-            jax.ShapeDtypeStruct((count // 2, entries), f32),
+            jax.ShapeDtypeStruct((3, SPREAD, width), f32),
+            jax.ShapeDtypeStruct((SPREAD, entries), f32),
             jax.ShapeDtypeStruct((2, entries), jnp.int32),
         ),
         in_specs=[smem, vmem, vmem, vmem],

time: 33.1 us -> 32.7 us (0.988)
  Pallas kernels: 10.7 us -> 9.63 us
  waiting for transfers between devices: 0.36 us -> 1.24 us
    all_to_all x1, waiting for transfers between devices: 0.36 us -> 1.24 us  [exchange(): lax.all_to_all(shaped, AXES, split_axis=0, concat_axis=0, tiled=True)]
    pallas_call x1, Pallas kernels: 6.81 us -> 6 us  [local(): pl.pallas_call(own_kernel, out_shape=jax.ShapeDtypeStruct((1, count), f32...]
  transfers between devices with their start and end apart: 1 -> 1, of which waited for: 1 -> 1; matrix products, arithmetic and copies ran while one was open for 0% -> 0% of each run, Pallas kernels for 22% -> 19%
where the time goes in v5:
time: 32.7 us
  blocking collectives  17.7 us (54%)
  Pallas kernels  9.63 us (29%)
  starting transfers between devices  2.69 us (8%)
  between operations  1.35 us (4%)
  waiting for transfers between devices  1.24 us (4%)
    all_to_all x1, blocking collectives, exchange(): lax.all_to_all(shaped, AXES, split_axis=0, concat_axis=0, tiled=True)  17.7 us
    pallas_call x1, Pallas kernels, local(): pl.pallas_call(own_kernel, out_shape=jax.ShapeDtypeStruct((1, count), f32...  6 us
    all_to_all x1, starting transfers between devices, exchange(): lax.all_to_all(shaped, AXES, split_axis=0, concat_axis=0, tiled=True)  2.69 us
    pallas_call x1, Pallas kernels, local(): pl.pallas_call(ghost_kernel, out_shape=[jax.ShapeDtypeStruct((1, count),...  1.49 us
    all_to_all x1, waiting for transfers between devices, exchange(): lax.all_to_all(shaped, AXES, split_axis=0, concat_axis=0, tiled=True)  1.24 us
    pallas_call x1, Pallas kernels, local(): pl.pallas_call(pack_kernel, out_shape=(jax.ShapeDtypeStruct((parts * SEND...  1.14 us
    pallas_call x1, Pallas kernels, local(): pl.pallas_call(select_kernel, out_shape=jax.ShapeDtypeStruct((parts * REP...  0.8 us
  transfers between devices with their start and end apart: 1, of which 1 were waited for; matrix products, arithmetic and copies ran while one was open for 0% of the time, Pallas kernels for 19%

profile of v5, /device:TPU:0, one launch (start us, length us, event | category | flops | bytes accessed | tf_op | source)
XLA Modules:
  0.0 32.7 jit_solution(4869450412182130437)
XLA Ops:
  0.6 1.1 %pack.1 = (f32[544,128]{1,0:T(8,128)S(1)}, f32[256,128]{1,0:T(8,128)S(1)}) custom-call(f32[12,64,128]{2,1,0:T(8,128)} %bitcast.14, s32[1,64]{1,0:T(1,128)} %bitcast.15, s32[1,16]{1,0:T(1,128)} %ghosts_hbm.1), custom_call_target="tpu_custom_call" | custom-call | tf_op jit(solution)/shard_map/pack/pallas_call | solution.py:249
  1.8 17.7 %all_to_all.10 = f32[32,17,1,128]{3,2,1,0:T(1,128)S(1)} all-to-all(f32[32,17,1,128]{3,2,1,0:T(1,128)S(1)} %bitcast.13), channel_id=1, replica_groups=mesh['gx'=4,'gy'=8] {'gx','gy'}, dimensions={0} | all-to-all | bytes 557056 | tf_op jit(solution)/shard_map/all_to_all | solution.py:235
  19.5 0.8 %select.1 = f32[256,128]{1,0:T(8,128)} custom-call(f32[544,128]{1,0:T(8,128)S(1)} %bitcast.10, f32[256,128]{1,0:T(8,128)S(1)} %get-tuple-element.12.table_ref), custom_call_target="tpu_custom_call" | custom-call | tf_op jit(solution)/shard_map/select/pallas_call | solution.py:280
  20.3 0.0 copy-start
  20.3 0.0 copy-start.1
  20.3 2.7 %all-to-all-start.1 = ((f32[32,8,1,128]{3,1,2,0:T(8,128)}), f32[32,8,1,128]{3,1,2,0:T(8,128)S(1)}, u32[]{:S(2)}, u32[]{:S(2)}) async-start(f32[32,8,1,128]{3,1,2,0:T(8,128)} %bitcast.5), calls=%async_computation.1 | async-start | bytes 262144 | tf_op jit(solution)/shard_map/all_to_all | solution.py:235
  23.0 0.0 copy-start.2
  23.7 0.0 copy-done
  23.7 0.0 copy-done.1
  23.7 0.0 copy-done.2
  23.7 0.2 prep.1
  23.9 6.0 %own.1.own_ref = f32[1,512]{1,0:T(1,128)S(1)} custom-call(f32[544,128]{1,0:T(8,128)S(1)} %bitcast.11, bf16[512,64]{1,0:T(8,128)(2,1)S(1)} %get-tuple-element.13.left_ref, f32[3,128,128]{2,1,0:T(8,128)S(1)} %get-tuple-element.14.spread_ref), custom_call_target="tpu_custom_call" | custom-call | flops 58720256 | bytes 278528 | tf_op jit(solution)/shard_map/own/pallas_call | solution.py:289
  29.9 1.2 %all-to-all-done.1 = f32[32,8,1,128]{3,1,2,0:T(8,128)S(1)} async-done(((f32[32,8,1,128]{3,1,2,0:T(8,128)}), f32[32,8,1,128]{3,1,2,0:T(8,128)S(1)}, u32[]{:S(2)}, u32[]{:S(2)}) %all-to-all-start.1) | async-done | bytes 131104 | tf_op jit(solution)/shard_map/all_to_all | solution.py:235
  31.2 1.5 %ghost.1 = (f32[1,512]{1,0:T(1,128)}, f32[1,512]{1,0:T(1,128)}) custom-call(s32[1]{0:T(128)S(6)} %copy.10.limit_ref, s32[2,16]{1,0:T(2,128)S(1)} %get-tuple-element.10.place_ref, f32[256,128]{1,0:T(8,128)S(1)} %bitcast.12, f32[3,512]{1,0:T(4,128)S(1)} %copy-done, bf16[512,64]{1,0:T(8,128)(2,1)S(1)} %get-tuple-element.13.left_ref, ...), custom_call_target="tpu_custom_call" | custom-call | tf_op jit(solution)/shard_map/ghost/pallas_call | solution.py:301
Async XLA Ops:
  20.3 3.4 %copy-start = (f32[3,512]{1,0:T(4,128)S(1)}, f32[3,512]{1,0:T(4,128)}, u32[]{:S(2)}) copy-start(f32[3,512]{1,0:T(4,128)} %nodes_ref.3) | copy-start | bytes 18436
  20.3 3.4 %copy-start.1 = (s32[4,512]{1,0:T(4,128)S(1)}, s32[4,512]{1,0:T(4,128)}, u32[]{:S(2)}) copy-start(s32[4,512]{1,0:T(4,128)} %cand_ref.1) | copy-start | bytes 24580
  20.3 10.9 %all-to-all-start.1 = ((f32[32,8,1,128]{3,1,2,0:T(8,128)}), f32[32,8,1,128]{3,1,2,0:T(8,128)S(1)}, u32[]{:S(2)}, u32[]{:S(2)}) async-start(f32[32,8,1,128]{3,1,2,0:T(8,128)} %bitcast.5), calls=%async_computation.1 | async-start | bytes 262144 | tf_op jit(solution)/shard_map/all_to_all | solution.py:235
  23.0 0.7 %copy-start.2 = (s32[1,16]{1,0:T(1,128)S(1)}, s32[1,16]{1,0:T(1,128)}, u32[]{:S(2)}) copy-start(s32[1,16]{1,0:T(1,128)} %ghosts_hbm.1) | copy-start | bytes 196

commit v6 on v5

--- a/solution.py
+++ b/solution.py
@@ -13,7 +13,7 @@
 OWN_ROWS = CAP * FEAT
 SEND_ROWS = OWN_ROWS + 1
 REPLY_ROWS = GC * FEAT
-UNROLL = 8
+UNROLL = 16
 CHUNK = 64
 GHOST_CHUNKS = 2
 SPREAD = 128
@@ -217,8 +217,8 @@
     for most in GHOST_LEVELS:
         some = min(most, entries)
         if some > least:
-            enough = limit_ref[0] > least if some == entries else (limit_ref[0] > least) & (limit_ref[0] <= some)
-            pl.when(enough)(functools.partial(some_entries, range(some)))
+            fits = limit_ref[0] > least if some == entries else limit_ref[0] <= some
+            pl.when(fits if least == 0 else fits & (limit_ref[0] > least))(functools.partial(some_entries, range(some)))
         least = some
     px, py, pz = [nodes_ref[c : c + 1, :] for c in range(3)]
     square = px * px + py * py + pz * pz

time: 32.7 us -> 32.8 us (level)
  Pallas kernels: 9.63 us -> 7.52 us
  waiting for transfers between devices: 1.24 us -> 3.34 us
    pallas_call x1, Pallas kernels: 6 us -> 3.89 us  [local(): pl.pallas_call(own_kernel, out_shape=jax.ShapeDtypeStruct((1, count), f32...]
    all_to_all x1, waiting for transfers between devices: 1.24 us -> 3.34 us  [exchange(): lax.all_to_all(shaped, AXES, split_axis=0, concat_axis=0, tiled=True)]
  transfers between devices with their start and end apart: 1 -> 1, of which waited for: 1 -> 1; matrix products, arithmetic and copies ran while one was open for 0% -> 0% of each run, Pallas kernels for 19% -> 13%
where the time goes in v6:
time: 32.8 us; the launch traced here: 32.6 us
  blocking collectives  17.7 us (54%)
  Pallas kernels  7.52 us (23%)
  waiting for transfers between devices  3.34 us (10%)
  starting transfers between devices  2.69 us (8%)
  between operations  1.35 us (4%)
    all_to_all x1, blocking collectives, exchange(): lax.all_to_all(shaped, AXES, split_axis=0, concat_axis=0, tiled=True)  17.7 us
    pallas_call x1, Pallas kernels, local(): pl.pallas_call(own_kernel, out_shape=jax.ShapeDtypeStruct((1, count), f32...  3.89 us
    all_to_all x1, waiting for transfers between devices, exchange(): lax.all_to_all(shaped, AXES, split_axis=0, concat_axis=0, tiled=True)  3.34 us
    all_to_all x1, starting transfers between devices, exchange(): lax.all_to_all(shaped, AXES, split_axis=0, concat_axis=0, tiled=True)  2.69 us
    pallas_call x1, Pallas kernels, local(): pl.pallas_call(ghost_kernel, out_shape=[jax.ShapeDtypeStruct((1, count),...  1.48 us
    pallas_call x1, Pallas kernels, local(): pl.pallas_call(pack_kernel, out_shape=(jax.ShapeDtypeStruct((parts * SEND...  1.14 us
    pallas_call x1, Pallas kernels, local(): pl.pallas_call(select_kernel, out_shape=jax.ShapeDtypeStruct((parts * REP...  0.8 us
  transfers between devices with their start and end apart: 1, of which 1 were waited for; matrix products, arithmetic and copies ran while one was open for 0% of the time, Pallas kernels for 13%

profile of v6, /device:TPU:0, one launch (start us, length us, event | category | flops | bytes accessed | tf_op | source)
XLA Modules:
  0.0 32.6 jit_solution(7465520869522462040)
XLA Ops:
  0.6 1.1 %pack.1 = (f32[544,128]{1,0:T(8,128)S(1)}, f32[256,128]{1,0:T(8,128)S(1)}) custom-call(f32[12,64,128]{2,1,0:T(8,128)} %bitcast.14, s32[1,64]{1,0:T(1,128)} %bitcast.15, s32[1,16]{1,0:T(1,128)} %ghosts_hbm.1), custom_call_target="tpu_custom_call" | custom-call | tf_op jit(solution)/shard_map/pack/pallas_call | solution.py:249
  1.8 17.7 %all_to_all.10 = f32[32,17,1,128]{3,2,1,0:T(1,128)S(1)} all-to-all(f32[32,17,1,128]{3,2,1,0:T(1,128)S(1)} %bitcast.13), channel_id=1, replica_groups=mesh['gx'=4,'gy'=8] {'gx','gy'}, dimensions={0} | all-to-all | bytes 557056 | tf_op jit(solution)/shard_map/all_to_all | solution.py:235
  19.5 0.8 %select.1 = f32[256,128]{1,0:T(8,128)} custom-call(f32[544,128]{1,0:T(8,128)S(1)} %bitcast.10, f32[256,128]{1,0:T(8,128)S(1)} %get-tuple-element.12.table_ref), custom_call_target="tpu_custom_call" | custom-call | tf_op jit(solution)/shard_map/select/pallas_call | solution.py:280
  20.3 0.0 copy-start
  20.3 0.0 copy-start.1
  20.3 2.7 %all-to-all-start.1 = ((f32[32,8,1,128]{3,1,2,0:T(8,128)}), f32[32,8,1,128]{3,1,2,0:T(8,128)S(1)}, u32[]{:S(2)}, u32[]{:S(2)}) async-start(f32[32,8,1,128]{3,1,2,0:T(8,128)} %bitcast.5), calls=%async_computation.1 | async-start | bytes 262144 | tf_op jit(solution)/shard_map/all_to_all | solution.py:235
  23.0 0.0 copy-start.2
  23.7 0.0 copy-done
  23.7 0.0 copy-done.1
  23.7 0.0 copy-done.2
  23.7 0.2 prep.1
  23.9 3.9 %own.1.own_ref = f32[1,512]{1,0:T(1,128)S(1)} custom-call(f32[544,128]{1,0:T(8,128)S(1)} %bitcast.11, bf16[512,64]{1,0:T(8,128)(2,1)S(1)} %get-tuple-element.13.left_ref, f32[3,128,128]{2,1,0:T(8,128)S(1)} %get-tuple-element.14.spread_ref), custom_call_target="tpu_custom_call" | custom-call | flops 58720256 | bytes 278528 | tf_op jit(solution)/shard_map/own/pallas_call | solution.py:289
  27.8 3.3 %all-to-all-done.1 = f32[32,8,1,128]{3,1,2,0:T(8,128)S(1)} async-done(((f32[32,8,1,128]{3,1,2,0:T(8,128)}), f32[32,8,1,128]{3,1,2,0:T(8,128)S(1)}, u32[]{:S(2)}, u32[]{:S(2)}) %all-to-all-start.1) | async-done | bytes 131104 | tf_op jit(solution)/shard_map/all_to_all | solution.py:235
  31.2 1.5 %ghost.1 = (f32[1,512]{1,0:T(1,128)}, f32[1,512]{1,0:T(1,128)}) custom-call(s32[1]{0:T(128)S(6)} %copy.10.limit_ref, s32[2,16]{1,0:T(2,128)S(1)} %get-tuple-element.10.place_ref, f32[256,128]{1,0:T(8,128)S(1)} %bitcast.12, f32[3,512]{1,0:T(4,128)S(1)} %copy-done, bf16[512,64]{1,0:T(8,128)(2,1)S(1)} %get-tuple-element.13.left_ref, ...), custom_call_target="tpu_custom_call" | custom-call | tf_op jit(solution)/shard_map/ghost/pallas_call | solution.py:301
Async XLA Ops:
  20.3 3.4 %copy-start = (f32[3,512]{1,0:T(4,128)S(1)}, f32[3,512]{1,0:T(4,128)}, u32[]{:S(2)}) copy-start(f32[3,512]{1,0:T(4,128)} %nodes_ref.3) | copy-start | bytes 18436
  20.3 3.4 %copy-start.1 = (s32[4,512]{1,0:T(4,128)S(1)}, s32[4,512]{1,0:T(4,128)}, u32[]{:S(2)}) copy-start(s32[4,512]{1,0:T(4,128)} %cand_ref.1) | copy-start | bytes 24580
  20.3 10.9 %all-to-all-start.1 = ((f32[32,8,1,128]{3,1,2,0:T(8,128)}), f32[32,8,1,128]{3,1,2,0:T(8,128)S(1)}, u32[]{:S(2)}, u32[]{:S(2)}) async-start(f32[32,8,1,128]{3,1,2,0:T(8,128)} %bitcast.5), calls=%async_computation.1 | async-start | bytes 262144 | tf_op jit(solution)/shard_map/all_to_all | solution.py:235
  23.0 0.7 %copy-start.2 = (s32[1,16]{1,0:T(1,128)S(1)}, s32[1,16]{1,0:T(1,128)}, u32[]{:S(2)}) copy-start(s32[1,16]{1,0:T(1,128)} %ghosts_hbm.1) | copy-start | bytes 196

commit v7 on v6

--- a/solution.py
+++ b/solution.py
@@ -15,9 +15,8 @@
 REPLY_ROWS = GC * FEAT
 UNROLL = 16
 CHUNK = 64
-GHOST_CHUNKS = 2
 SPREAD = 128
-GHOST_LEVELS = (4, 8, 1 << 30)
+GHOST_LEVELS = (2, 4, 8, 12, 1 << 30)
 AXES = ("gx", "gy")
 
 far_gap = 10.0
@@ -109,7 +108,7 @@
     return [high, middle, low, high, middle, high]
 
 
-def prep_kernel(limit_ref, wanted_ref, nodes_ref, cand_ref, left_ref, spread_ref, shade_ref, place_ref, *, blocks):
+def prep_kernel(limit_ref, wanted_ref, nodes_ref, cand_ref, left_ref, right_ref, spread_ref, place_ref, *, blocks):
     count = nodes_ref.shape[1]
     _, spread_count, width = spread_ref.shape
     start = count - spread_count
@@ -127,8 +126,9 @@
     for k in range(1, cand_ref.shape[0]):
         chosen = chosen | (entry == cand_ref[k : k + 1, :])
     mask = jnp.where(chosen & (entry < limit_ref[0]), 0.0, penalty)
-    left_ref[...] = jnp.concatenate(point_terms(nodes_ref[...]) + [mask], axis=0).T.astype(jnp.bfloat16)
-    shade_ref[...] = mask[:, start:].T
+    right = jnp.concatenate(point_terms(nodes_ref[...]) + [mask], axis=0)
+    right_ref[...] = right.astype(jnp.bfloat16)
+    left_ref[...] = right.T.astype(jnp.bfloat16)
     for c in range(3):
         for g in range(spread_count // width):
             row = nodes_ref[c : c + 1, start + g * width : start + (g + 1) * width]
@@ -177,41 +177,25 @@
         out_ref[:, here] = jnp.min(best_ref[here, :].T, axis=0, keepdims=True)
 
 
-def ghost_kernel(
-    limit_ref, place_ref, reply_ref, nodes_ref, left_ref, spread_ref, shade_ref, own_ref, own_out_ref, out_ref, best_ref
-):
+def ghost_kernel(limit_ref, place_ref, reply_ref, nodes_ref, right_ref, own_ref, own_out_ref, out_ref, best_ref):
     entries = place_ref.shape[1]
     count = nodes_ref.shape[1]
     width = reply_ref.shape[1]
-    spread_start = count - spread_ref.shape[1]
-    first = count - GHOST_CHUNKS * CHUNK
     place = place_ref[...]
     slot = lax.broadcasted_iota(jnp.int32, (2 * FEAT, width), 0) // FEAT
     choice = lax.broadcasted_iota(jnp.int32, (entries, width), 0)
 
     def some_entries(members):
-        sides = []
-        starts = []
+        best = None
         for e in members:
             start, order = place[0, e], place[1, e]
-            starts.append(start + order * FEAT)
             tile = reply_ref[pl.ds(pl.multiple_of(start, REPLY_ROWS), REPLY_ROWS), :]
             kept = jnp.where(slot == order, tile, 0.0)
-            rows = stack_terms(*split3(kept)) + [to_one(choice == e).astype(jnp.bfloat16)]
-            sides.append(jnp.concatenate(rows, axis=0))
-        gaps = jnp.dot(left_ref[0:first, :], jnp.concatenate(sides, axis=1), preferred_element_type=jnp.float32)
-        best_ref[0:first, :] = functools.reduce(
-            jnp.minimum, [gaps[:, i * width : (i + 1) * width] for i in range(len(sides))]
-        )
-        for j in range(first, count, CHUNK):
-            here = slice(j - spread_start, j - spread_start + CHUNK)
-            x, y, z = [spread_ref[c, here, :] for c in range(3)]
-            least = jnp.full((CHUNK, width), penalty, jnp.float32)
-            for e, start in zip(members, starts):
-                lx, ly, lz, off = [reply_ref[pl.ds(start + c, 1), :] for c in range(FEAT)]
-                shade = jnp.broadcast_to(shade_ref[here, e : e + 1], (CHUNK, width))
-                least = jnp.minimum(least, ((x * lx + y * ly) + (z * lz + off)) + shade)
-            best_ref[j : j + CHUNK, :] = least
+            rows = jnp.concatenate(stack_terms(*split3(kept)) + [to_one(choice == e).astype(jnp.bfloat16)], axis=0)
+            gaps = jnp.dot(rows.T, right_ref[...], preferred_element_type=jnp.float32)
+            least = jnp.min(gaps.reshape(width // 8, 8, count), axis=0)
+            best = least if best is None else jnp.minimum(best, least)
+        best_ref[...] = best
 
     least = 0
     for most in GHOST_LEVELS:
@@ -223,10 +207,7 @@
     px, py, pz = [nodes_ref[c : c + 1, :] for c in range(3)]
     square = px * px + py * py + pz * pz
     own_out_ref[...] = own_ref[...] + square
-    for g in range(count // width):
-        here = slice(g * width, (g + 1) * width)
-        least = jnp.min(best_ref[here, :].T, axis=0, keepdims=True)
-        out_ref[:, here] = jnp.minimum(far_gap, least + square[:, here])
+    out_ref[...] = jnp.minimum(far_gap, jnp.min(best_ref[...], axis=0, keepdims=True) + square)
 
 
 def exchange(rows, parts):
@@ -264,12 +245,12 @@
         compiler_params=params,
     )(*[pltpu.with_memory_space_constraint(v, pltpu.HBM) for v in (jnp.transpose(facets, (1, 0, 2)), owner.T, ghosts)])
     arrived = exchange(outgoing, parts)
-    left, spread, shade, place = pl.pallas_call(
+    left, right, spread, place = pl.pallas_call(
         functools.partial(prep_kernel, blocks=blocks),
         out_shape=(
             jax.ShapeDtypeStruct((count, 6 * 2 * FEAT + entries), jnp.bfloat16),
+            jax.ShapeDtypeStruct((6 * 2 * FEAT + entries, count), jnp.bfloat16),
             jax.ShapeDtypeStruct((3, SPREAD, width), f32),
-            jax.ShapeDtypeStruct((SPREAD, entries), f32),
             jax.ShapeDtypeStruct((2, entries), jnp.int32),
         ),
         in_specs=[smem, vmem, vmem, vmem],
@@ -301,12 +282,12 @@
     own_gap, ghost_gap = pl.pallas_call(
         ghost_kernel,
         out_shape=[jax.ShapeDtypeStruct((1, count), f32)] * 2,
-        in_specs=[smem] + [vmem] * 7,
+        in_specs=[smem] + [vmem] * 5,
         out_specs=[vmem, vmem],
-        scratch_shapes=[pltpu.VMEM((count, width), f32)],
+        scratch_shapes=[pltpu.VMEM((8, count), f32)],
         name="ghost",
         compiler_params=params,
-    )(ghost_count, place, reply, nodes, left, spread, shade, own_least)
+    )(ghost_count, place, reply, nodes, right, own_least)
     return own_gap.reshape(count), ghost_gap.reshape(count)
 
 

time: 32.8 us -> 32.8 us (level)
  no operation moved by 1% of the time
where the time goes in v7:
time: 32.8 us; the launch traced here: 32.5 us
  blocking collectives  17.7 us (54%)
  Pallas kernels  7.47 us (23%)
  waiting for transfers between devices  3.26 us (10%)
  starting transfers between devices  2.69 us (8%)
  between operations  1.35 us (4%)
    all_to_all x1, blocking collectives, exchange(): lax.all_to_all(shaped, AXES, split_axis=0, concat_axis=0, tiled=True)  17.7 us
    pallas_call x1, Pallas kernels, local(): pl.pallas_call(own_kernel, out_shape=jax.ShapeDtypeStruct((1, count), f32...  3.98 us
    all_to_all x1, waiting for transfers between devices, exchange(): lax.all_to_all(shaped, AXES, split_axis=0, concat_axis=0, tiled=True)  3.26 us
    all_to_all x1, starting transfers between devices, exchange(): lax.all_to_all(shaped, AXES, split_axis=0, concat_axis=0, tiled=True)  2.69 us
    pallas_call x1, Pallas kernels, local(): pl.pallas_call(ghost_kernel, out_shape=[jax.ShapeDtypeStruct((1, count),...  1.35 us
    pallas_call x1, Pallas kernels, local(): pl.pallas_call(pack_kernel, out_shape=(jax.ShapeDtypeStruct((parts * SEND...  1.14 us
    pallas_call x1, Pallas kernels, local(): pl.pallas_call(select_kernel, out_shape=jax.ShapeDtypeStruct((parts * REP...  0.8 us
  transfers between devices with their start and end apart: 1, of which 1 were waited for; matrix products, arithmetic and copies ran while one was open for 0% of the time, Pallas kernels for 13%

profile of v7, /device:TPU:0, one launch (start us, length us, event | category | flops | bytes accessed | tf_op | source)
XLA Modules:
  0.0 32.5 jit_solution(10186229848471453763)
XLA Ops:
  0.6 1.1 %pack.1 = (f32[544,128]{1,0:T(8,128)S(1)}, f32[256,128]{1,0:T(8,128)S(1)}) custom-call(f32[12,64,128]{2,1,0:T(8,128)} %bitcast.14, s32[1,64]{1,0:T(1,128)} %bitcast.15, s32[1,16]{1,0:T(1,128)} %ghosts_hbm.1), custom_call_target="tpu_custom_call" | custom-call | tf_op jit(solution)/shard_map/pack/pallas_call | solution.py:230
  1.8 17.7 %all_to_all.10 = f32[32,17,1,128]{3,2,1,0:T(1,128)S(1)} all-to-all(f32[32,17,1,128]{3,2,1,0:T(1,128)S(1)} %bitcast.13), channel_id=1, replica_groups=mesh['gx'=4,'gy'=8] {'gx','gy'}, dimensions={0} | all-to-all | bytes 557056 | tf_op jit(solution)/shard_map/all_to_all | solution.py:216
  19.5 0.8 %select.1 = f32[256,128]{1,0:T(8,128)} custom-call(f32[544,128]{1,0:T(8,128)S(1)} %bitcast.10, f32[256,128]{1,0:T(8,128)S(1)} %get-tuple-element.12.table_ref), custom_call_target="tpu_custom_call" | custom-call | tf_op jit(solution)/shard_map/select/pallas_call | solution.py:261
  20.3 0.0 copy-start
  20.3 0.0 copy-start.1
  20.3 2.7 %all-to-all-start.1 = ((f32[32,8,1,128]{3,1,2,0:T(8,128)}), f32[32,8,1,128]{3,1,2,0:T(8,128)S(1)}, u32[]{:S(2)}, u32[]{:S(2)}) async-start(f32[32,8,1,128]{3,1,2,0:T(8,128)} %bitcast.5), calls=%async_computation.1 | async-start | bytes 262144 | tf_op jit(solution)/shard_map/all_to_all | solution.py:216
  23.0 0.0 copy-start.2
  23.7 0.0 copy-done
  23.7 0.0 copy-done.1
  23.7 0.0 copy-done.2
  23.7 0.2 prep.1
  23.9 4.0 %own.1.own_ref = f32[1,512]{1,0:T(1,128)S(1)} custom-call(f32[544,128]{1,0:T(8,128)S(1)} %bitcast.11, bf16[512,64]{1,0:T(8,128)(2,1)S(1)} %get-tuple-element.14.left_ref, f32[3,128,128]{2,1,0:T(8,128)S(1)} %get-tuple-element.15.spread_ref), custom_call_target="tpu_custom_call" | custom-call | flops 58720256 | bytes 278528 | tf_op jit(solution)/shard_map/own/pallas_call | solution.py:270
  27.9 3.3 %all-to-all-done.1 = f32[32,8,1,128]{3,1,2,0:T(8,128)S(1)} async-done(((f32[32,8,1,128]{3,1,2,0:T(8,128)}), f32[32,8,1,128]{3,1,2,0:T(8,128)S(1)}, u32[]{:S(2)}, u32[]{:S(2)}) %all-to-all-start.1) | async-done | bytes 131104 | tf_op jit(solution)/shard_map/all_to_all | solution.py:216
  31.2 1.3 %ghost.1 = (f32[1,512]{1,0:T(1,128)}, f32[1,512]{1,0:T(1,128)}) custom-call(s32[1]{0:T(128)S(6)} %copy.10.limit_ref, s32[2,16]{1,0:T(2,128)S(1)} %get-tuple-element.10.place_ref, f32[256,128]{1,0:T(8,128)S(1)} %bitcast.12, f32[3,512]{1,0:T(4,128)S(1)} %copy-done, bf16[64,512]{1,0:T(8,128)(2,1)S(1)} %get-tuple-element.13.right_ref, f32[1,512]{1,0:T(1,128)S(1)} %own.1.own_ref), custom_call_target="tpu_custom_call" | custom-call | tf_op jit(solution)/shard_map/ghost/pallas_call | solution.py:282
Async XLA Ops:
  20.3 3.4 %copy-start = (f32[3,512]{1,0:T(4,128)S(1)}, f32[3,512]{1,0:T(4,128)}, u32[]{:S(2)}) copy-start(f32[3,512]{1,0:T(4,128)} %nodes_ref.3) | copy-start | bytes 18436
  20.3 3.4 %copy-start.1 = (s32[4,512]{1,0:T(4,128)S(1)}, s32[4,512]{1,0:T(4,128)}, u32[]{:S(2)}) copy-start(s32[4,512]{1,0:T(4,128)} %cand_ref.1) | copy-start | bytes 24580
  20.3 10.9 %all-to-all-start.1 = ((f32[32,8,1,128]{3,1,2,0:T(8,128)}), f32[32,8,1,128]{3,1,2,0:T(8,128)S(1)}, u32[]{:S(2)}, u32[]{:S(2)}) async-start(f32[32,8,1,128]{3,1,2,0:T(8,128)} %bitcast.5), calls=%async_computation.1 | async-start | bytes 262144 | tf_op jit(solution)/shard_map/all_to_all | solution.py:216
  23.0 0.7 %copy-start.2 = (s32[1,16]{1,0:T(1,128)S(1)}, s32[1,16]{1,0:T(1,128)}, u32[]{:S(2)}) copy-start(s32[1,16]{1,0:T(1,128)} %ghosts_hbm.1) | copy-start | bytes 196

commit v8 on v6

--- a/solution.py
+++ b/solution.py
@@ -17,7 +17,8 @@
 CHUNK = 64
 GHOST_CHUNKS = 2
 SPREAD = 128
-GHOST_LEVELS = (4, 8, 1 << 30)
+GHOST_LEVELS = (2, 4, 8, 12, 1 << 30)
+FEW = 8
 AXES = ("gx", "gy")
 
 far_gap = 10.0
@@ -109,7 +110,7 @@
     return [high, middle, low, high, middle, high]
 
 
-def prep_kernel(limit_ref, wanted_ref, nodes_ref, cand_ref, left_ref, spread_ref, shade_ref, place_ref, *, blocks):
+def prep_kernel(limit_ref, wanted_ref, nodes_ref, cand_ref, left_ref, right_ref, spread_ref, shade_ref, place_ref, *, blocks):
     count = nodes_ref.shape[1]
     _, spread_count, width = spread_ref.shape
     start = count - spread_count
@@ -127,7 +128,9 @@
     for k in range(1, cand_ref.shape[0]):
         chosen = chosen | (entry == cand_ref[k : k + 1, :])
     mask = jnp.where(chosen & (entry < limit_ref[0]), 0.0, penalty)
-    left_ref[...] = jnp.concatenate(point_terms(nodes_ref[...]) + [mask], axis=0).T.astype(jnp.bfloat16)
+    right = jnp.concatenate(point_terms(nodes_ref[...]) + [mask], axis=0)
+    right_ref[...] = right.astype(jnp.bfloat16)
+    left_ref[...] = right.T.astype(jnp.bfloat16)
     shade_ref[...] = mask[:, start:].T
     for c in range(3):
         for g in range(spread_count // width):
@@ -178,7 +181,7 @@
 
 
 def ghost_kernel(
-    limit_ref, place_ref, reply_ref, nodes_ref, left_ref, spread_ref, shade_ref, own_ref, own_out_ref, out_ref, best_ref
+    limit_ref, place_ref, reply_ref, nodes_ref, left_ref, right_ref, spread_ref, shade_ref, own_ref, own_out_ref, out_ref, best_ref
 ):
     entries = place_ref.shape[1]
     count = nodes_ref.shape[1]
@@ -188,6 +191,21 @@
     place = place_ref[...]
     slot = lax.broadcasted_iota(jnp.int32, (2 * FEAT, width), 0) // FEAT
     choice = lax.broadcasted_iota(jnp.int32, (entries, width), 0)
+
+    px, py, pz = [nodes_ref[c : c + 1, :] for c in range(3)]
+    square = px * px + py * py + pz * pz
+    own_out_ref[...] = own_ref[...] + square
+
+    def few_entries(members):
+        best = []
+        for e in members:
+            tile = reply_ref[pl.ds(pl.multiple_of(place[0, e], REPLY_ROWS), REPLY_ROWS), :]
+            kept = jnp.where(slot == place[1, e], tile, 0.0)
+            rows = jnp.concatenate(stack_terms(*split3(kept)) + [to_one(choice == e).astype(jnp.bfloat16)], axis=0)
+            gaps = jnp.dot(rows.T, right_ref[...], preferred_element_type=jnp.float32)
+            best.append(jnp.min(gaps.reshape(width // 8, 8, count), axis=0))
+        least = jnp.min(functools.reduce(jnp.minimum, best), axis=0, keepdims=True)
+        out_ref[...] = jnp.minimum(far_gap, least + square)
 
     def some_entries(members):
         sides = []
@@ -212,21 +230,20 @@
                 shade = jnp.broadcast_to(shade_ref[here, e : e + 1], (CHUNK, width))
                 least = jnp.minimum(least, ((x * lx + y * ly) + (z * lz + off)) + shade)
             best_ref[j : j + CHUNK, :] = least
+        for g in range(count // width):
+            here = slice(g * width, (g + 1) * width)
+            least = jnp.min(best_ref[here, :].T, axis=0, keepdims=True)
+            out_ref[:, here] = jnp.minimum(far_gap, least + square[:, here])
 
     least = 0
     for most in GHOST_LEVELS:
         some = min(most, entries)
         if some > least:
             fits = limit_ref[0] > least if some == entries else limit_ref[0] <= some
-            pl.when(fits if least == 0 else fits & (limit_ref[0] > least))(functools.partial(some_entries, range(some)))
+            pl.when(fits if least == 0 else fits & (limit_ref[0] > least))(
+                functools.partial(few_entries if some <= FEW else some_entries, range(some))
+            )
         least = some
-    px, py, pz = [nodes_ref[c : c + 1, :] for c in range(3)]
-    square = px * px + py * py + pz * pz
-    own_out_ref[...] = own_ref[...] + square
-    for g in range(count // width):
-        here = slice(g * width, (g + 1) * width)
-        least = jnp.min(best_ref[here, :].T, axis=0, keepdims=True)
-        out_ref[:, here] = jnp.minimum(far_gap, least + square[:, here])
 
 
 def exchange(rows, parts):
@@ -264,16 +281,17 @@
         compiler_params=params,
     )(*[pltpu.with_memory_space_constraint(v, pltpu.HBM) for v in (jnp.transpose(facets, (1, 0, 2)), owner.T, ghosts)])
     arrived = exchange(outgoing, parts)
-    left, spread, shade, place = pl.pallas_call(
+    left, right, spread, shade, place = pl.pallas_call(
         functools.partial(prep_kernel, blocks=blocks),
         out_shape=(
             jax.ShapeDtypeStruct((count, 6 * 2 * FEAT + entries), jnp.bfloat16),
+            jax.ShapeDtypeStruct((6 * 2 * FEAT + entries, count), jnp.bfloat16),
             jax.ShapeDtypeStruct((3, SPREAD, width), f32),
             jax.ShapeDtypeStruct((SPREAD, entries), f32),
             jax.ShapeDtypeStruct((2, entries), jnp.int32),
         ),
         in_specs=[smem, vmem, vmem, vmem],
-        out_specs=(vmem, vmem, vmem, vmem),
+        out_specs=(vmem,) * 5,
         name="prep",
         compiler_params=params,
     )(ghost_count, ghosts, nodes, cand)
@@ -301,12 +319,12 @@
     own_gap, ghost_gap = pl.pallas_call(
         ghost_kernel,
         out_shape=[jax.ShapeDtypeStruct((1, count), f32)] * 2,
-        in_specs=[smem] + [vmem] * 7,
+        in_specs=[smem] + [vmem] * 8,
         out_specs=[vmem, vmem],
         scratch_shapes=[pltpu.VMEM((count, width), f32)],
         name="ghost",
         compiler_params=params,
-    )(ghost_count, place, reply, nodes, left, spread, shade, own_least)
+    )(ghost_count, place, reply, nodes, left, right, spread, shade, own_least)
     return own_gap.reshape(count), ghost_gap.reshape(count)
 
 

time: 32.8 us -> 32.7 us (level)
  no operation moved by 1% of the time
where the time goes in v8:
time: 32.7 us; the launch traced here: 32.6 us
  blocking collectives  17.7 us (54%)
  Pallas kernels  7.48 us (23%)
  waiting for transfers between devices  3.34 us (10%)
  starting transfers between devices  2.69 us (8%)
  between operations  1.35 us (4%)
    all_to_all x1, blocking collectives, exchange(): lax.all_to_all(shaped, AXES, split_axis=0, concat_axis=0, tiled=True)  17.7 us
    pallas_call x1, Pallas kernels, local(): pl.pallas_call(own_kernel, out_shape=jax.ShapeDtypeStruct((1, count), f32...  3.89 us
    all_to_all x1, waiting for transfers between devices, exchange(): lax.all_to_all(shaped, AXES, split_axis=0, concat_axis=0, tiled=True)  3.34 us
    all_to_all x1, starting transfers between devices, exchange(): lax.all_to_all(shaped, AXES, split_axis=0, concat_axis=0, tiled=True)  2.69 us
    pallas_call x1, Pallas kernels, local(): pl.pallas_call(ghost_kernel, out_shape=[jax.ShapeDtypeStruct((1, count),...  1.43 us
    pallas_call x1, Pallas kernels, local(): pl.pallas_call(pack_kernel, out_shape=(jax.ShapeDtypeStruct((parts * SEND...  1.14 us
    pallas_call x1, Pallas kernels, local(): pl.pallas_call(select_kernel, out_shape=jax.ShapeDtypeStruct((parts * REP...  0.8 us
  transfers between devices with their start and end apart: 1, of which 1 were waited for; matrix products, arithmetic and copies ran while one was open for 0% of the time, Pallas kernels for 13%

profile of v8, /device:TPU:0, one launch (start us, length us, event | category | flops | bytes accessed | tf_op | source)
XLA Modules:
  0.0 32.6 jit_solution(247958139585597943)
XLA Ops:
  0.6 1.1 %pack.1 = (f32[544,128]{1,0:T(8,128)S(1)}, f32[256,128]{1,0:T(8,128)S(1)}) custom-call(f32[12,64,128]{2,1,0:T(8,128)} %bitcast.14, s32[1,64]{1,0:T(1,128)} %bitcast.15, s32[1,16]{1,0:T(1,128)} %ghosts_hbm.1), custom_call_target="tpu_custom_call" | custom-call | tf_op jit(solution)/shard_map/pack/pallas_call | solution.py:266
  1.8 17.7 %all_to_all.10 = f32[32,17,1,128]{3,2,1,0:T(1,128)S(1)} all-to-all(f32[32,17,1,128]{3,2,1,0:T(1,128)S(1)} %bitcast.13), channel_id=1, replica_groups=mesh['gx'=4,'gy'=8] {'gx','gy'}, dimensions={0} | all-to-all | bytes 557056 | tf_op jit(solution)/shard_map/all_to_all | solution.py:252
  19.5 0.8 %select.1 = f32[256,128]{1,0:T(8,128)} custom-call(f32[544,128]{1,0:T(8,128)S(1)} %bitcast.10, f32[256,128]{1,0:T(8,128)S(1)} %get-tuple-element.13.table_ref), custom_call_target="tpu_custom_call" | custom-call | tf_op jit(solution)/shard_map/select/pallas_call | solution.py:298
  20.3 0.0 copy-start
  20.3 0.0 copy-start.1
  20.3 2.7 %all-to-all-start.1 = ((f32[32,8,1,128]{3,1,2,0:T(8,128)}), f32[32,8,1,128]{3,1,2,0:T(8,128)S(1)}, u32[]{:S(2)}, u32[]{:S(2)}) async-start(f32[32,8,1,128]{3,1,2,0:T(8,128)} %bitcast.5), calls=%async_computation.1 | async-start | bytes 262144 | tf_op jit(solution)/shard_map/all_to_all | solution.py:252
  23.0 0.0 copy-start.2
  23.7 0.0 copy-done
  23.7 0.0 copy-done.1
  23.7 0.0 copy-done.2
  23.7 0.2 prep.1
  23.9 3.9 %own.1.own_ref = f32[1,512]{1,0:T(1,128)S(1)} custom-call(f32[544,128]{1,0:T(8,128)S(1)} %bitcast.11, bf16[512,64]{1,0:T(8,128)(2,1)S(1)} %get-tuple-element.14.left_ref, f32[3,128,128]{2,1,0:T(8,128)S(1)} %get-tuple-element.16.spread_ref), custom_call_target="tpu_custom_call" | custom-call | flops 58720256 | bytes 278528 | tf_op jit(solution)/shard_map/own/pallas_call | solution.py:307
  27.8 3.3 %all-to-all-done.1 = f32[32,8,1,128]{3,1,2,0:T(8,128)S(1)} async-done(((f32[32,8,1,128]{3,1,2,0:T(8,128)}), f32[32,8,1,128]{3,1,2,0:T(8,128)S(1)}, u32[]{:S(2)}, u32[]{:S(2)}) %all-to-all-start.1) | async-done | bytes 131104 | tf_op jit(solution)/shard_map/all_to_all | solution.py:252
  31.2 1.4 %ghost.1 = (f32[1,512]{1,0:T(1,128)}, f32[1,512]{1,0:T(1,128)}) custom-call(s32[1]{0:T(128)S(6)} %copy.10.limit_ref, s32[2,16]{1,0:T(2,128)S(1)} %get-tuple-element.11.place_ref, f32[256,128]{1,0:T(8,128)S(1)} %bitcast.12, f32[3,512]{1,0:T(4,128)S(1)} %copy-done, bf16[512,64]{1,0:T(8,128)(2,1)S(1)} %get-tuple-element.14.left_ref, ...), custom_call_target="tpu_custom_call" | custom-call | tf_op jit(solution)/shard_map/ghost/pallas_call | solution.py:319
Async XLA Ops:
  20.3 3.4 %copy-start = (f32[3,512]{1,0:T(4,128)S(1)}, f32[3,512]{1,0:T(4,128)}, u32[]{:S(2)}) copy-start(f32[3,512]{1,0:T(4,128)} %nodes_ref.3) | copy-start | bytes 18436
  20.3 3.4 %copy-start.1 = (s32[4,512]{1,0:T(4,128)S(1)}, s32[4,512]{1,0:T(4,128)}, u32[]{:S(2)}) copy-start(s32[4,512]{1,0:T(4,128)} %cand_ref.1) | copy-start | bytes 24580
  20.3 10.9 %all-to-all-start.1 = ((f32[32,8,1,128]{3,1,2,0:T(8,128)}), f32[32,8,1,128]{3,1,2,0:T(8,128)S(1)}, u32[]{:S(2)}, u32[]{:S(2)}) async-start(f32[32,8,1,128]{3,1,2,0:T(8,128)} %bitcast.5), calls=%async_computation.1 | async-start | bytes 262144 | tf_op jit(solution)/shard_map/all_to_all | solution.py:252
  23.0 0.7 %copy-start.2 = (s32[1,16]{1,0:T(1,128)S(1)}, s32[1,16]{1,0:T(1,128)}, u32[]{:S(2)}) copy-start(s32[1,16]{1,0:T(1,128)} %ghosts_hbm.1) | copy-start | bytes 196

commit v9 on v8

--- a/solution.py
+++ b/solution.py
@@ -14,6 +14,7 @@
 SEND_ROWS = OWN_ROWS + 1
 REPLY_ROWS = GC * FEAT
 UNROLL = 16
+PIECES = 2
 CHUNK = 64
 GHOST_CHUNKS = 2
 SPREAD = 128
@@ -91,13 +92,22 @@
         out_ref[pl.ds(starts[b], FEAT), :] = table_ref[b * FEAT : (b + 1) * FEAT, :]
 
 
-def select_kernel(arrived_ref, table_ref, out_ref):
+def select_kernel(arrived_ref, table_ref, out_hbm, rows_ref, sems):
     parts = arrived_ref.shape[0] // SEND_ROWS
     request = arrived_ref[pl.ds(OWN_ROWS, parts, stride=SEND_ROWS), :].astype(jnp.int32) * FEAT
-    for d in range(parts):
-        for s in range(GC):
-            row = d * REPLY_ROWS + s * FEAT
-            out_ref[row : row + FEAT, :] = table_ref[pl.ds(pl.multiple_of(request[d, s], FEAT), FEAT), :]
+    pieces = sems.shape[0]
+    share = parts // pieces
+    sends = []
+    for piece in range(pieces):
+        for d in range(piece * share, (piece + 1) * share):
+            for s in range(GC):
+                row = d * REPLY_ROWS + s * FEAT
+                rows_ref[row : row + FEAT, :] = table_ref[pl.ds(pl.multiple_of(request[d, s], FEAT), FEAT), :]
+        here = pl.ds(piece * share * REPLY_ROWS, share * REPLY_ROWS)
+        sends.append(pltpu.make_async_copy(rows_ref.at[here], out_hbm.at[here], sems.at[piece]))
+        sends[-1].start()
+    for send in sends:
+        send.wait()
 
 
 def stack_terms(high, middle, low):
@@ -299,7 +309,8 @@
         select_kernel,
         out_shape=jax.ShapeDtypeStruct((parts * REPLY_ROWS, width), f32),
         in_specs=[vmem, vmem],
-        out_specs=vmem,
+        out_specs=hbm,
+        scratch_shapes=[pltpu.VMEM((parts * REPLY_ROWS, width), f32), pltpu.SemaphoreType.DMA((PIECES,))],
         name="select",
         compiler_params=params,
     )(arrived, table)

time: 32.7 us -> 32.6 us (level)
  no operation moved by 1% of the time
where the time goes in v9:
time: 32.6 us; the launch traced here: 32.3 us
  blocking collectives  17.7 us (54%)
  Pallas kernels  7.26 us (22%)
  waiting for transfers between devices  3.33 us (10%)
  starting transfers between devices  2.64 us (8%)
  between operations  1.38 us (4%)
    all_to_all x1, blocking collectives, exchange(): lax.all_to_all(shaped, AXES, split_axis=0, concat_axis=0, tiled=True)  17.7 us
    pallas_call x1, Pallas kernels, local(): pl.pallas_call(own_kernel, out_shape=jax.ShapeDtypeStruct((1, count), f32...  3.9 us
    all_to_all x1, waiting for transfers between devices, exchange(): lax.all_to_all(shaped, AXES, split_axis=0, concat_axis=0, tiled=True)  3.33 us
    all_to_all x1, starting transfers between devices, exchange(): lax.all_to_all(shaped, AXES, split_axis=0, concat_axis=0, tiled=True)  2.64 us
    pallas_call x1, Pallas kernels, local(): pl.pallas_call(ghost_kernel, out_shape=[jax.ShapeDtypeStruct((1, count),...  1.21 us
    pallas_call x1, Pallas kernels, local(): pl.pallas_call(pack_kernel, out_shape=(jax.ShapeDtypeStruct((parts * SEND...  1.14 us
    pallas_call x1, Pallas kernels, local(): pl.pallas_call(select_kernel, out_shape=jax.ShapeDtypeStruct((parts * REP...  0.79 us
  transfers between devices with their start and end apart: 1, of which 1 were waited for; matrix products, arithmetic and copies ran while one was open for 0% of the time, Pallas kernels for 13%

profile of v9, /device:TPU:0, one launch (start us, length us, event | category | flops | bytes accessed | tf_op | source)
XLA Modules:
  0.0 32.3 jit_solution(3354471332902376962)
XLA Ops:
  0.6 1.1 %pack.1 = (f32[544,128]{1,0:T(8,128)S(1)}, f32[256,128]{1,0:T(8,128)S(1)}) custom-call(f32[12,64,128]{2,1,0:T(8,128)} %bitcast.14, s32[1,64]{1,0:T(1,128)} %bitcast.15, s32[1,16]{1,0:T(1,128)} %ghosts_hbm.1), custom_call_target="tpu_custom_call" | custom-call | tf_op jit(solution)/shard_map/pack/pallas_call | solution.py:276
  1.8 17.7 %all_to_all.10 = f32[32,17,1,128]{3,2,1,0:T(1,128)S(1)} all-to-all(f32[32,17,1,128]{3,2,1,0:T(1,128)S(1)} %bitcast.13), channel_id=1, replica_groups=mesh['gx'=4,'gy'=8] {'gx','gy'}, dimensions={0} | all-to-all | bytes 557056 | tf_op jit(solution)/shard_map/all_to_all | solution.py:262
  19.5 0.8 %select.1 = f32[256,128]{1,0:T(8,128)} custom-call(f32[544,128]{1,0:T(8,128)S(1)} %bitcast.10, f32[256,128]{1,0:T(8,128)S(1)} %get-tuple-element.13.table_ref), custom_call_target="tpu_custom_call" | custom-call | tf_op jit(solution)/shard_map/select/pallas_call | solution.py:308
  20.3 0.0 copy-start
  20.3 0.0 copy-start.1
  20.3 2.6 %all-to-all-start.1 = ((f32[32,8,1,128]{3,1,2,0:T(8,128)}), f32[32,8,1,128]{3,1,2,0:T(8,128)S(1)}, u32[]{:S(2)}, u32[]{:S(2)}) async-start(f32[32,8,1,128]{3,1,2,0:T(8,128)} %bitcast.5), calls=%async_computation.1 | async-start | bytes 262144 | tf_op jit(solution)/shard_map/all_to_all | solution.py:262
  23.0 0.0 copy-start.2
  23.6 0.0 copy-done
  23.7 0.0 copy-done.1
  23.7 0.0 copy-done.2
  23.7 0.2 prep.1
  23.9 3.9 %own.1.own_ref = f32[1,512]{1,0:T(1,128)S(1)} custom-call(f32[544,128]{1,0:T(8,128)S(1)} %bitcast.11, bf16[512,64]{1,0:T(8,128)(2,1)S(1)} %get-tuple-element.14.left_ref, f32[3,128,128]{2,1,0:T(8,128)S(1)} %get-tuple-element.16.spread_ref), custom_call_target="tpu_custom_call" | custom-call | flops 58720256 | bytes 278528 | tf_op jit(solution)/shard_map/own/pallas_call | solution.py:318
  27.8 3.3 %all-to-all-done.1 = f32[32,8,1,128]{3,1,2,0:T(8,128)S(1)} async-done(((f32[32,8,1,128]{3,1,2,0:T(8,128)}), f32[32,8,1,128]{3,1,2,0:T(8,128)S(1)}, u32[]{:S(2)}, u32[]{:S(2)}) %all-to-all-start.1) | async-done | bytes 131104 | tf_op jit(solution)/shard_map/all_to_all | solution.py:262
  31.1 1.2 %ghost.1 = (f32[1,512]{1,0:T(1,128)}, f32[1,512]{1,0:T(1,128)}) custom-call(s32[1]{0:T(128)S(6)} %copy.10.limit_ref, s32[2,16]{1,0:T(2,128)S(1)} %get-tuple-element.11.place_ref, f32[256,128]{1,0:T(8,128)S(1)} %bitcast.12, f32[3,512]{1,0:T(4,128)S(1)} %copy-done, bf16[512,64]{1,0:T(8,128)(2,1)S(1)} %get-tuple-element.14.left_ref, ...), custom_call_target="tpu_custom_call" | custom-call | tf_op jit(solution)/shard_map/ghost/pallas_call | solution.py:330
Async XLA Ops:
  20.3 3.3 %copy-start = (f32[3,512]{1,0:T(4,128)S(1)}, f32[3,512]{1,0:T(4,128)}, u32[]{:S(2)}) copy-start(f32[3,512]{1,0:T(4,128)} %nodes_ref.3) | copy-start | bytes 18436
  20.3 3.3 %copy-start.1 = (s32[4,512]{1,0:T(4,128)S(1)}, s32[4,512]{1,0:T(4,128)}, u32[]{:S(2)}) copy-start(s32[4,512]{1,0:T(4,128)} %cand_ref.1) | copy-start | bytes 24580
  20.3 10.8 %all-to-all-start.1 = ((f32[32,8,1,128]{3,1,2,0:T(8,128)}), f32[32,8,1,128]{3,1,2,0:T(8,128)S(1)}, u32[]{:S(2)}, u32[]{:S(2)}) async-start(f32[32,8,1,128]{3,1,2,0:T(8,128)} %bitcast.5), calls=%async_computation.1 | async-start | bytes 262144 | tf_op jit(solution)/shard_map/all_to_all | solution.py:262
  23.0 0.7 %copy-start.2 = (s32[1,16]{1,0:T(1,128)S(1)}, s32[1,16]{1,0:T(1,128)}, u32[]{:S(2)}) copy-start(s32[1,16]{1,0:T(1,128)} %ghosts_hbm.1) | copy-start | bytes 196
